TPU v7x, 32 devices: a whole 2x2x4 slice. The times are simulated.
32 devices in a mesh: seq: 8 (over y, x, core), head: 4 (over z).
Axes of the slice: x: 2, y: 2, z: 4, core: 2. Of those that a mesh axis runs over, the one named last changes fastest.
Arguments:
- query_rows: bfloat16 [2048, 1024], P('seq', 'head'), may hold values from -6 to 6
- key_rows: bfloat16 [2048, 1024], P('seq', 'head'), may hold values from -6 to 6
- value_rows: bfloat16 [2048, 2048], P('seq', 'head'), may hold values from -6 to 6
- output_gate: bfloat16 [2048, 2048], P('seq', 'head'), may hold values from -6 to 6
- write_rate: float32 [16, 2048], P('head', 'seq'), may hold values from 0.05 to 1
- log_decay: float32 [16, 2048], P('head', 'seq'), may hold values from -1.2 to 0, as said below
- out_weight: bfloat16 [2048, 2048], P(None, 'head'), may hold values from -0.125 to 0.125
- out_cotangent: bfloat16 [2048, 2048], P('seq', 'head'), may hold values from -6 to 6
- block_response: int32 [24], replicated, may hold values from 0 to 15, as said below
- prefix_owner: int32 [8], replicated, may hold values from 0 to 7, each once
Outputs:
- layer_out: bfloat16 [2048, 2048], P('seq', 'head')
- grad_query: float32 [2048, 1024], P('seq', 'head')
- grad_key: float32 [2048, 1024], P('seq', 'head')
- grad_value: float32 [2048, 2048], P('seq', 'head')
- grad_gate: float32 [2048, 2048], P('seq', 'head')
- grad_write: float32 [16, 2048], P('head', 'seq')
- grad_decay: float32 [16, 2048], P('head', 'seq')
- grad_weight: float32 [2048, 2048], P('seq', 'head')
Inputs may be any that keep to these rules, and one draw needn't show every extreme that they name: `block_response`: blocks of one response are consecutive and lie within the 3 blocks of one index of seq; responses appear in increasing order; each response has 1 to 3 blocks and one has exactly 3; every response of 0 to 15 appears. `prefix_owner`: each index of seq holds exactly one prompt's prefix. `log_decay`: every entry is negative.
All inputs are finite; a program needn't handle non-finite values.
Results may differ from a plain program's by a relative error of at most 0.015.
Values may be sent and summed in bfloat16 or wider, within the bound.
No kernel may reach another device: no remote copies, remote signals or barrier semaphores. Data moves between devices by JAX's collectives and lax.ppermute only.
A program may use at most 64 MiB of HBM per device.

v0:
```python
from functools import partial

import jax
import jax.numpy as jnp
from jax import lax
from jax.sharding import PartitionSpec as P

DK = 128
DV = 128
SPAN = 64
PREFIX = 64
BLK_DEV = 3
RESP_PER = 2


highest = lax.Precision.HIGHEST
tiny_eps = 1e-06


def unit_rows(raw_rows):
    return raw_rows * lax.rsqrt(jnp.sum(raw_rows * raw_rows, axis=-1, keepdims=True) + tiny_eps)


def span_parts(query_unit, key_unit, value_part, write_part, decay_part):
    span_len = decay_part.shape[-1]
    dim_key = key_unit.shape[-1]
    cumulative = jnp.cumsum(decay_part, axis=-1)
    row_ids = lax.broadcasted_iota(jnp.int32, (span_len, span_len), 0)
    col_ids = lax.broadcasted_iota(jnp.int32, (span_len, span_len), 1)
    strict = row_ids > col_ids
    causal = row_ids >= col_ids
    spread = cumulative[..., :, None] - cumulative[..., None, :]
    below_diag = jnp.where(strict, jnp.exp(jnp.where(strict, spread, 0.0)), 0.0)
    within = jnp.where(causal, jnp.exp(jnp.where(causal, spread, 0.0)), 0.0)
    key_key = jnp.einsum("...ik,...jk->...ij", key_unit, key_unit, precision=highest)
    system = jnp.eye(span_len, dtype=jnp.float32) + write_part[..., :, None] * below_diag * key_key
    growth = jnp.exp(cumulative)
    right_side = jnp.concatenate(
        [(write_part * growth)[..., None] * key_unit, write_part[..., None] * value_part], axis=-1
    )
    solved = lax.linalg.triangular_solve(
        system, right_side, left_side=True, lower=True, unit_diagonal=True
    )
    weights_w = solved[..., :dim_key]
    base_u = solved[..., dim_key:]
    query_key = jnp.einsum("...ik,...jk->...ij", query_unit, key_unit, precision=highest) * within
    remain = jnp.exp(cumulative[..., -1:] - cumulative)
    key_tail = remain[..., None] * key_unit
    transfer = growth[..., -1][..., None, None] * jnp.eye(dim_key, dtype=jnp.float32) - jnp.einsum(
        "...ck,...cl->...kl", weights_w, key_tail, precision=highest
    )
    offset = jnp.einsum("...cv,...ck->...vk", base_u, key_tail, precision=highest)
    return (transfer, offset, weights_w, base_u, query_key, growth, query_unit)


def span_apply(span_terms, state_in):
    transfer, offset, weights_w, base_u, query_key, growth, query_unit = span_terms
    update = base_u - jnp.einsum("...ck,...vk->...cv", weights_w, state_in, precision=highest)
    block_out = growth[..., None] * jnp.einsum(
        "...ck,...vk->...cv", query_unit, state_in, precision=highest
    )
    block_out = block_out + jnp.einsum("...ij,...jv->...iv", query_key, update, precision=highest)
    state_out = jnp.einsum("...vk,...kl->...vl", state_in, transfer, precision=highest) + offset
    return (block_out, state_out)


def split_heads(flat_rows, feat_width):
    return jnp.transpose(flat_rows.reshape(flat_rows.shape[0], -1, feat_width), (1, 0, 2))


def blocks_first(head_array):
    heads_count, row_total, feat_width = head_array.shape
    return jnp.transpose(
        head_array.reshape(heads_count, row_total // SPAN, SPAN, feat_width), (1, 0, 2, 3)
    )


def heads_first(block_array):
    block_total, heads_count, span_len, feat_width = block_array.shape
    return jnp.transpose(block_array, (1, 0, 2, 3)).reshape(
        heads_count, block_total * span_len, feat_width
    )


def region_inputs(query32, key32, value32, write_part, decay_part):
    heads_count = write_part.shape[0]
    query_unit = unit_rows(split_heads(query32, DK)) * DK ** (-0.5)
    key_unit = unit_rows(split_heads(key32, DK))
    repeat_by = heads_count // query_unit.shape[0]
    query_unit = jnp.repeat(query_unit, repeat_by, axis=0)
    key_unit = jnp.repeat(key_unit, repeat_by, axis=0)
    values = split_heads(value32, DV)
    return (
        blocks_first(query_unit),
        blocks_first(key_unit),
        blocks_first(values),
        blocks_first(write_part[..., None])[..., 0],
        blocks_first(decay_part[..., None])[..., 0],
    )


def prefix_pass(query32, key32, value32, write_part, decay_part):
    heads_count = write_part.shape[0]

    def prefix_advance(state_in, block_in):
        block_out, state_out = span_apply(span_parts(*block_in), state_in)
        return (state_out, block_out)

    last_state, block_outs = lax.scan(
        prefix_advance,
        jnp.zeros((heads_count, DV, DK), jnp.float32),
        region_inputs(query32, key32, value32, write_part, decay_part),
    )
    return (block_outs, last_state)


def answer_parts(query32, key32, value32, write_part, decay_part):
    return span_parts(*region_inputs(query32, key32, value32, write_part, decay_part))


def respond_blocks(span_terms, states_all, carry_in, block_flags, owners):

    def respond_advance(state_in, block_in):
        terms_here, block_flag, block_owner = block_in
        chosen = lax.dynamic_index_in_dim(states_all, block_owner, 0, keepdims=False)
        state_in = jnp.where(block_flag, chosen, state_in)
        block_out, state_out = span_apply(terms_here, state_in)
        return (state_out, block_out)

    ignored, block_outs = lax.scan(respond_advance, carry_in, (span_terms, block_flags, owners))
    return block_outs


def gated_norm(outs_all, gate32):
    inv_scale = lax.rsqrt(jnp.mean(outs_all * outs_all, axis=-1, keepdims=True) + tiny_eps)
    gated_rows = outs_all * inv_scale * jax.nn.silu(split_heads(gate32, DV))
    return jnp.transpose(gated_rows, (1, 0, 2)).reshape(gate32.shape[0], -1)


def per_device(
    query_rows,
    key_rows,
    value_rows,
    output_gate,
    write_rate,
    log_decay,
    out_weight,
    out_cotangent,
    block_response,
    prefix_owner,
):
    query32 = query_rows.astype(jnp.float32)
    key32 = key_rows.astype(jnp.float32)
    value32 = value_rows.astype(jnp.float32)
    gate32 = output_gate.astype(jnp.float32)
    heads_count = write_rate.shape[0]
    block_ids = lax.axis_index("seq") * BLK_DEV + jnp.arange(BLK_DEV, dtype=jnp.int32)
    current = jnp.take(block_response, block_ids)
    previous = jnp.take(block_response, jnp.maximum(block_ids - 1, 0))
    block_flags = (block_ids == 0) | (current != previous)
    owners = jnp.take(prefix_owner, current // RESP_PER)
    prefix_in = (
        query32[:PREFIX],
        key32[:PREFIX],
        value32[:PREFIX],
        write_rate[:, :PREFIX],
        log_decay[:, :PREFIX],
    )
    answer_in = (
        query32[PREFIX:],
        key32[PREFIX:],
        value32[PREFIX:],
        write_rate[:, PREFIX:],
        log_decay[:, PREFIX:],
    )
    (prefix_outs, prefix_last), prefix_pull = jax.vjp(prefix_pass, *prefix_in)
    shared = lax.all_gather(prefix_last.astype(jnp.bfloat16)[None], "seq", axis=0, tiled=True)
    states_all = shared.astype(jnp.float32)
    span_terms, terms_pull = jax.vjp(answer_parts, *answer_in)
    zero_state = jnp.zeros((heads_count, DV, DK), jnp.float32)
    respond = partial(respond_blocks, carry_in=zero_state, block_flags=block_flags, owners=owners)
    answer_outs, answer_pull = jax.vjp(respond, span_terms, states_all)
    outs_all = jnp.concatenate([heads_first(prefix_outs), heads_first(answer_outs)], axis=1)
    normed, norm_pull = jax.vjp(gated_norm, outs_all, gate32)
    rounded = normed.astype(jnp.bfloat16)
    partial_out = jnp.einsum("rv,dv->rd", rounded, out_weight, preferred_element_type=jnp.float32)
    layer_out = lax.psum_scatter(partial_out, "head", scatter_dimension=1, tiled=True).astype(
        jnp.bfloat16
    )
    cotangent = lax.all_gather(out_cotangent, "head", axis=1, tiled=True)
    grad_normed = jnp.dot(cotangent, out_weight, preferred_element_type=jnp.float32)
    grad_weight = lax.psum_scatter(
        jnp.einsum("rd,rv->dv", cotangent, rounded, preferred_element_type=jnp.float32).astype(
            jnp.bfloat16
        ),
        "seq",
        scatter_dimension=0,
        tiled=True,
    ).astype(jnp.float32)
    grad_outs, grad_gate = norm_pull(grad_normed)
    grad_prefix = blocks_first(grad_outs[:, :PREFIX])
    grad_answer = blocks_first(grad_outs[:, PREFIX:])
    grad_terms, grad_states = answer_pull(grad_answer)
    pieces = lax.all_to_all(
        grad_states.astype(jnp.bfloat16), "seq", split_axis=0, concat_axis=0, tiled=True
    ).astype(grad_states.dtype)
    own_state = jnp.sum(pieces, axis=0)
    prefix_grads = prefix_pull((grad_prefix, own_state))
    answer_grads = terms_pull(grad_terms)
    grad_query = jnp.concatenate([prefix_grads[0], answer_grads[0]], axis=0)
    grad_key = jnp.concatenate([prefix_grads[1], answer_grads[1]], axis=0)
    grad_value = jnp.concatenate([prefix_grads[2], answer_grads[2]], axis=0)
    grad_write = jnp.concatenate([prefix_grads[3], answer_grads[3]], axis=1)
    grad_decay = jnp.concatenate([prefix_grads[4], answer_grads[4]], axis=1)
    return (
        layer_out,
        grad_query,
        grad_key,
        grad_value,
        grad_gate,
        grad_write,
        grad_decay,
        grad_weight,
    )


def solution(mesh):
    placed = (
        P("seq", "head"),
        P("seq", "head"),
        P("seq", "head"),
        P("seq", "head"),
        P("head", "seq"),
        P("head", "seq"),
        P(None, "head"),
        P("seq", "head"),
        P(),
        P(),
    )
    return jax.shard_map(
        per_device,
        mesh=mesh,
        in_specs=placed,
        out_specs=(
            P("seq", "head"),
            P("seq", "head"),
            P("seq", "head"),
            P("seq", "head"),
            P("seq", "head"),
            P("head", "seq"),
            P("head", "seq"),
            P("seq", "head"),
        ),
        check_vma=False,
    )
```

profile of v0, /device:TPU:0, one launch (start us, length us, event | category | flops | bytes accessed | tf_op | source)
XLA Modules:
  0.0 393.8 jit_solution(7803396645725117313)
XLA Ops:
  12.6 19.6 %custom-call.22 = f32[4,1,64,64]{2,3,1,0:T(8,128)S(1)} custom-call(f32[4,1,64,64]{3,2,1,0:T(8,128)S(1)} %fusion.196), custom_call_target="InvertDiagBlocksLowerTriangular" | custom-call | tf_op jit(solution)/shard_map/jvp()/while/body/eval_jaxpr/triangular_solve | solution.py:41
  55.4 2.4 fusion.106
  57.9 60.3 %custom-call.23 = f32[3,4,1,64,64]{3,4,2,1,0:T(8,128)} custom-call(f32[3,4,1,64,64]{4,3,2,1,0:T(8,128)} %get-tuple-element.1590), custom_call_target="InvertDiagBlocksLowerTriangular" | custom-call | tf_op jit(solution)/shard_map/jvp()/triangular_solve | solution.py:41
  124.4 2.4 fusion.121
  126.8 2.5 convolution_subtract_fusion.1
  129.4 2.2 fusion.325
  132.5 2.8 convert.22
  137.7 64.0 %while.17 = (s32[]{:T(128)}, f32[4,128,128]{2,1,0:T(8,128)}, f32[3,4,64,128]{3,2,1,0:T(8,128)}, s32[3]{0:T(128)}, f32[3,4,128,128]{3,2,1,0:T(8,128)S(1)}, /*inde...) while((s32[]{:T(128)}, f32[4,128,128]{2,1,0:T(8,128)}, ...), condition=%wide.region_7.9_spmd.clone.clone, body=%wide.region_6.8_spmd.clone.sunk.clone | while | flops 226787328 | bytes 4074760 | solution.py:130
  146.8 2.1 convolution_add_fusion.24
  148.9 2.2 bitcast_dynamic-update-slice_fusion.17
  151.1 2.2 bitcast_dynamic-update-slice_fusion.16
  164.4 2.1 convolution_add_fusion.24
  166.5 2.2 bitcast_dynamic-update-slice_fusion.17
  168.7 2.2 bitcast_dynamic-update-slice_fusion.16
  181.8 2.1 convolution_add_fusion.24
  184.0 2.2 bitcast_dynamic-update-slice_fusion.17
  186.1 2.2 bitcast_dynamic-update-slice_fusion.16
  212.9 60.9 %while.18 = (s32[]{:T(128)}, f32[8,4,128,128]{2,3,1,0:T(8,128)}, f32[4,128,128]{1,2,0:T(8,128)S(1)}, f32[3,4,128,128]{3,2,1,0:T(8,128)}, f32[3,4,128,128]{2,3,1,...) while((s32[]{:T(128)}, f32[8,4,128,128]{2,3,1,0:T(8,128)}, ...), condition=%wide.region_15.17_spmd.clone.clone, body=%wide.region_13.16_spmd.clone.sunk.clone | while | flops 453705472 | bytes 10112291 | solution.py:130
  228.9 3.6 fusion.434
  249.2 3.6 fusion.434
  269.5 3.6 fusion.434
  274.5 3.7 fusion.312
  286.3 3.4 fusion.66
  289.8 2.2 convolution_add_fusion.6
  292.1 4.1 %fusion.101 = (f32[3,4,64,64]{3,2,1,0:T(8,128)}, f32[3,4,64]{2,1,0:T(4,128)}, f32[3,4,64,64]{3,2,1,0:T(8,128)}) fusion(f32[3,4,64,64]{3,2,1,0:T(8,128)} %fusion.115, f32[3,4,64,64]{3,2,1,0:T(8,128)} %copy-done.28, f32[3,4,64]{2,1,0:T(4,128)S(1)} %reduce_window_sum.53, f32[3,4,64]{2,1,0:T(4,128)} %bitcast.741, pred[64,64]{1,0:T(8,128)(4,1)} %copy-done.64, ...), kind=kOutput, calls=%fused_computation.167 | convolution fusion | flops 38632704 | bytes 1397760 | tf_op jit(solution)/shard_map/transpose(jvp())/triangular_solve | solution.py:41
  299.2 2.3 convolution_add_fusion.8
  309.2 3.4 reduce_window_sum.56
  314.3 2.8 convert_element_type.90
  317.2 5.3 %all-to-all-start = ((bf16[8,4,128,128]{2,3,1,0:T(8,128)(2,1)}), bf16[8,4,128,128]{2,3,1,0:T(8,128)(2,1)}, u32[]{:S(2)}, u32[]{:S(2)}) async-start(bf16[8,4,128,128]{2,3,1,0:T(8,128)(2,1)} %convert_element_type.90), calls=%async_computation.1 | async-start | bytes 2097152 | tf_op jit(solution)/shard_map/all_to_all | solution.py:204
  344.2 2.1 multiply_reduce_fusion.3
  349.7 2.3 multiply_reduce_fusion.6
  377.9 7.4 %reduce-scatter.3.cloned.1.call-done = f32[256,512]{1,0:T(8,128)} async-done(((f32[256,2048]{1,0:T(8,128)}), f32[256,512]{1,0:T(8,128)}) %reduce-scatter.3.cloned.1.call-update) | async-done | bytes 524304 | tf_op jit(solution)/shard_map/reduce_scatter | solution.py:187
  (452 shorter events, 199.1 us)
Async XLA Ops:
  7.2 122.2 %copy-start = (bf16[2048,512]{1,0:T(8,128)(2,1)S(1)}, bf16[2048,512]{1,0:T(8,128)(2,1)}, u32[]{:S(2)}) copy-start(bf16[2048,512]{1,0:T(8,128)(2,1)} %param.22) | copy-start | bytes 6291460
  7.2 25.1 %copy-start.40 = (bf16[256,512]{1,0:T(8,128)(2,1)S(1)}, bf16[256,512]{1,0:T(8,128)(2,1)}, u32[]{:S(2)}) copy-start(bf16[256,512]{1,0:T(8,128)(2,1)} %param.18) | copy-start | bytes 786436
  7.2 122.2 %all-gather.4.cloned.1.call-start = ((), (), s32[]{:S(2)}) async-start(), calls=%async_computation.4 | async-start | bytes 1310720 | tf_op jit(solution)/shard_map/all_gather | solution.py:190
  7.9 124.6 %all-gather.6.cloned.1.call-start = ((), (), s32[]{:S(2)}) async-start(), calls=%async_computation.6 | async-start | bytes 1179648 | tf_op jit(solution)/shard_map/all_gather | solution.py:177
  9.2 25.0 %copy-start.78 = (pred[64,64]{1,0:T(8,128)(4,1)}, pred[64,64]{1,0:T(8,128)(4,1)S(1)}, u32[]{:S(2)}) copy-start(pred[64,64]{1,0:T(8,128)(4,1)S(1)} %get-tuple-element.1617) | copy-start | bytes 12292
  9.2 46.2 %copy-start.68 = (pred[64,64]{1,0:T(8,128)(4,1)}, pred[64,64]{1,0:T(8,128)(4,1)S(1)}, u32[]{:S(2)}) copy-start(pred[64,64]{1,0:T(8,128)(4,1)S(1)} %get-tuple-element.1616) | copy-start | bytes 12292
  10.1 31.8 %copy-start.12 = (f32[256,256]{1,0:T(8,128)}, f32[256,256]{1,0:T(8,128)S(1)}, u32[]{:S(2)}) copy-start(f32[256,256]{1,0:T(8,128)S(1)} %convert_element_type.80) | copy-start | bytes 786436
  10.4 31.0 %copy-start.9 = (f32[2,2,64,128]{3,2,1,0:T(8,128)}, f32[2,2,64,128]{3,2,1,0:T(8,128)S(1)}, u32[]{:S(2)}) copy-start(f32[2,2,64,128]{3,2,1,0:T(8,128)S(1)} %broadcast_in_dim.416) | copy-start | bytes 393220
  11.9 23.9 %copy-start.82 = (f32[4,64]{1,0:T(4,128)}, f32[4,64]{1,0:T(4,128)S(1)}, u32[]{:S(2)}) copy-start(f32[4,64]{1,0:T(4,128)S(1)} %get-tuple-element.1603) | copy-start | bytes 3076
  11.9 23.9 %copy-start.84 = (f32[4,64]{1,0:T(4,128)}, f32[4,64]{1,0:T(4,128)S(1)}, u32[]{:S(2)}) copy-start(f32[4,64]{1,0:T(4,128)S(1)} %get-tuple-element.1604) | copy-start | bytes 3076
  12.0 23.9 %copy-start.86 = (f32[4,64]{1,0:T(4,128)}, f32[4,64]{1,0:T(4,128)S(1)}, u32[]{:S(2)}) copy-start(f32[4,64]{1,0:T(4,128)S(1)} %get-tuple-element.1597) | copy-start | bytes 3076
  12.6 23.7 %copy-start.94 = (f32[4,256]{1,0:T(4,128)S(1)}, f32[4,256]{1,0:T(4,128)}, u32[]{:S(2)}) copy-start(f32[4,256]{1,0:T(4,128)} %param.21) | copy-start | bytes 12292
  12.6 23.8 %copy-start.91 = (f32[4,256]{1,0:T(4,128)S(1)}, f32[4,256]{1,0:T(4,128)}, u32[]{:S(2)}) copy-start(f32[4,256]{1,0:T(4,128)} %param.20) | copy-start | bytes 12292
  32.7 94.1 %copy-start.43 = (f32[128,128]{1,0:T(8,128)}, f32[128,128]{1,0:T(8,128)S(1)}, u32[]{:S(2)}) copy-start(f32[128,128]{1,0:T(8,128)S(1)} %fusion.273) | copy-start | bytes 196612
  33.5 13.2 %copy-start.18 = (f32[4,64,256]{2,1,0:T(8,128)}, f32[4,64,256]{2,1,0:T(8,128)S(1)}, u32[]{:S(2)}) copy-start(f32[4,64,256]{2,1,0:T(8,128)S(1)} %fusion.125) | copy-start | bytes 786436
  35.9 340.2 %reduce-scatter.5.cloned.1.call-start = ((), (), s32[]{:S(2)}) async-start(), calls=%async_computation.5 | async-start | bytes 2359296 | tf_op jit(solution)/shard_map/reduce_scatter | solution.py:192
  38.7 82.7 %copy-start.75 = (f32[4,3,64,1]{2,0,1,3:T(4,128)}, f32[4,3,64,1]{2,0,1,3:T(4,128)S(1)}, u32[]{:S(2)}) copy-start(f32[4,3,64,1]{2,0,1,3:T(4,128)S(1)} %copy.506) | copy-start | bytes 9220
  38.7 79.5 %copy-start.64 = (pred[64,64]{1,0:T(8,128)(4,1)}, pred[64,64]{1,0:T(8,128)(4,1)S(1)}, u32[]{:S(2)}) copy-start(pred[64,64]{1,0:T(8,128)(4,1)S(1)} %iota_compare_fusion.5) | copy-start | bytes 12292
  41.7 76.5 %copy-start.36 = (f32[4,64,64]{2,1,0:T(8,128)}, f32[4,64,64]{2,1,0:T(8,128)S(1)}, u32[]{:S(2)}) copy-start(f32[4,64,64]{2,1,0:T(8,128)S(1)} %fusion.322) | copy-start | bytes 196612
  49.6 68.6 %copy-start.61 = (f32[4,64,128]{2,1,0:T(8,128)S(1)}, f32[4,64,128]{2,1,0:T(8,128)}, u32[]{:S(2)}) copy-start(f32[4,64,128]{2,1,0:T(8,128)} %convolution_subtract_fusion.3) | copy-start | bytes 393220
  50.9 75.9 %copy-start.70 = (f32[3,4,64]{2,1,0:T(4,128)}, f32[3,4,64]{2,1,0:T(4,128)S(1)}, u32[]{:S(2)}) copy-start(f32[3,4,64]{2,1,0:T(4,128)S(1)} %get-tuple-element.1591) | copy-start | bytes 9220
  55.4 67.8 %copy-start.26 = (f32[192,4,128]{2,1,0:T(4,128)}, f32[192,4,128]{2,1,0:T(4,128)S(1)}, u32[]{:S(2)}) copy-start(f32[192,4,128]{2,1,0:T(4,128)S(1)} %reshape.644) | copy-start | bytes 1179652
  212.9 12.9 %copy-start.4 = (f32[3,4,128,128]{3,2,1,0:T(8,128)S(1)}, f32[3,4,128,128]{3,2,1,0:T(8,128)}, u32[]{:S(2)}) copy-start(f32[3,4,128,128]{3,2,1,0:T(8,128)} %get-tuple-element.2088) | copy-start | bytes 2359300 | tf_op jit(solution)/shard_map/transpose(jvp())/while
  233.2 12.9 %copy-start.4 = (f32[3,4,128,128]{3,2,1,0:T(8,128)S(1)}, f32[3,4,128,128]{3,2,1,0:T(8,128)}, u32[]{:S(2)}) copy-start(f32[3,4,128,128]{3,2,1,0:T(8,128)} %get-tuple-element.2088) | copy-start | bytes 2359300 | tf_op jit(solution)/shard_map/transpose(jvp())/while
  253.5 12.9 %copy-start.4 = (f32[3,4,128,128]{3,2,1,0:T(8,128)S(1)}, f32[3,4,128,128]{3,2,1,0:T(8,128)}, u32[]{:S(2)}) copy-start(f32[3,4,128,128]{3,2,1,0:T(8,128)} %get-tuple-element.2088) | copy-start | bytes 2359300 | tf_op jit(solution)/shard_map/transpose(jvp())/while
  317.2 12.1 %copy-start.15 = (f32[256,256]{1,0:T(8,128)S(1)}, f32[256,256]{1,0:T(8,128)}, u32[]{:S(2)}) copy-start(f32[256,256]{1,0:T(8,128)} %copy-done.14) | copy-start | bytes 786436
  317.2 14.5 %copy-start.37 = (f32[4,64,64]{2,1,0:T(8,128)S(1)}, f32[4,64,64]{2,1,0:T(8,128)}, u32[]{:S(2)}) copy-start(f32[4,64,64]{2,1,0:T(8,128)} %copy-done.36) | copy-start | bytes 196612
  317.2 14.5 %copy-start.67 = (pred[64,64]{1,0:T(8,128)(4,1)S(1)}, pred[64,64]{1,0:T(8,128)(4,1)}, u32[]{:S(2)}) copy-start(pred[64,64]{1,0:T(8,128)(4,1)} %copy-done.64) | copy-start | bytes 12292
  317.2 15.6 %copy-start.35 = (bf16[256,4,128]{0,2,1:T(8,128)(2,1)S(1)}, bf16[256,4,128]{0,2,1:T(8,128)(2,1)}, u32[]{:S(2)}) copy-start(bf16[256,4,128]{0,2,1:T(8,128)(2,1)} %copy-done.34) | copy-start | bytes 786436
  317.2 23.6 %all-to-all-start = ((bf16[8,4,128,128]{2,3,1,0:T(8,128)(2,1)}), bf16[8,4,128,128]{2,3,1,0:T(8,128)(2,1)}, u32[]{:S(2)}, u32[]{:S(2)}) async-start(bf16[8,4,128,128]{2,3,1,0:T(8,128)(2,1)} %convert_element_type.90), calls=%async_computation.1 | async-start | bytes 2097152 | tf_op jit(solution)/shard_map/all_to_all | solution.py:204
  322.5 62.8 %reduce-scatter.3.cloned.1.call-start = ((), (), s32[]{:S(2)}) async-start(), calls=%async_computation.3 | async-start | bytes 2621440 | tf_op jit(solution)/shard_map/reduce_scatter | solution.py:187
  364.0 11.2 %copy-start.69 = (f32[4,8,8,128]{3,2,0,1:T(8,128)S(1)}, f32[4,8,8,128]{3,2,0,1:T(8,128)}, u32[]{:S(2)}) copy-start(f32[4,8,8,128]{3,2,0,1:T(8,128)} %copy.505) | copy-start | bytes 393220
  (78 other events, 354.5 us)
Sparse Core Ops, SparseCore 0:
  9.6 30.7 all-gather.3
  42.8 22.8 all-gather.5
  289.9 48.1 reduce-scatter.4
  340.2 44.9 reduce-scatter.2
where the time goes:
time: 394 us
  other arithmetic  147 us (37%)
  matrix products  131 us (33%)
  local copies, waits for them, and re-layouts  67.9 us (17%)
  loops' own time  17.6 us (4%)
  between operations  15.4 us (4%)
  waiting for transfers between devices  8.62 us (2%)
  starting transfers between devices  5.87 us (1%)
    another operation x4, other arithmetic, span_parts(): lax.linalg.triangular_solve(system, right_side, left_side=True, lower=Tru...  80.1 us
    dot_general x11, matrix products, span_apply(): jnp.einsum('...ck,...vk->...cv', weights_w, state_in, precision=highest)  22.4 us
    dot_general x12, matrix products, span_apply(): jnp.einsum('...ij,...jv->...iv', query_key, update, precision=highest)  19.5 us
    dot_general x11, matrix products, span_apply(): jnp.einsum('...ck,...vk->...cv', query_unit, state_in, precision=highest)  19 us
    another operation x2, loops' own time, respond_blocks(): lax.scan(respond_advance, carry_in, (span_terms, block_flags, owners))  17.6 us
    dot_general x11, matrix products, span_apply(): jnp.einsum('...vk,...kl->...vl', state_in, transfer, precision=highest)  16.8 us
    dynamic_slice x12, local copies, waits for them, and re-layouts, respond_blocks(): lax.scan(respond_advance, carry_in, (span_terms, block_flags, owners))  15.1 us
    dot_general x6, matrix products, span_parts(): jnp.einsum('...cv,...ck->...vk', base_u, key_tail, precision=highest)  11.3 us
  transfers between devices with their start and end apart: 5, of which 2 were waited for; matrix products, arithmetic and copies ran while one was open for 51% of the time, Pallas kernels for 0%

commit v1 on v0

v1 whole, which is shorter than its diff:
```python
from functools import partial

import jax
import jax.numpy as jnp
from jax import lax
from jax.experimental import pallas as pl
from jax.experimental.pallas import tpu as pltpu
from jax.sharding import PartitionSpec as P

DK = 128
DV = 128
SPAN = 64
RESP_PER = 2
EPS = 1e-06
F32 = jnp.float32
BF16 = jnp.bfloat16
ROW_G, ROW_B, ROW_RK, ROW_RQ, ROW_END = 0, 8, 16, 24, 32


def dot_nn(a, b):
    return lax.dot_general(a, b, (((1,), (0,)), ((), ())), preferred_element_type=F32)


def dot_nt(a, b):
    return lax.dot_general(a, b, (((1,), (1,)), ((), ())), preferred_element_type=F32)


def dot_tn(a, b):
    return lax.dot_general(a, b, (((0,), (0,)), ((), ())), preferred_element_type=F32)


def halves(x):
    high = x.astype(BF16)
    return high, (x - high.astype(F32)).astype(BF16)


def dot3(a, b):
    ah, al = halves(a)
    bh, bl = halves(b)
    return dot_nn(ah, bh) + (dot_nn(ah, bl) + dot_nn(al, bh))


def iota2(shape, dim):
    return lax.broadcasted_iota(jnp.int32, shape, dim)


def unit_lower_inverse(lower, upto):
    size = lower.shape[0]
    ri, ci = iota2(lower.shape, 0), iota2(lower.shape, 1)
    eye = (ri == ci).astype(F32)
    inv = eye - jnp.where((ri // 2) == (ci // 2), lower, 0.0)
    step = 2
    while step < upto:
        joins = ((ri // (2 * step)) == (ci // (2 * step))) & ((ri // step) != (ci // step))
        off = jnp.where(joins, lower, 0.0).astype(BF16)
        inv16 = inv.astype(BF16)
        inv = inv - dot_nn(inv16, dot_nn(off, inv16).astype(BF16))
        step *= 2
    residual = (eye - inv) - dot3(lower, inv)
    return inv + dot_nn(inv.astype(BF16), residual.astype(BF16))


def response_ids(br_ref, blocks):
    base = lax.axis_index("seq") * blocks
    return [br_ref[base + b] for b in range(blocks)]


def segment_of(pos, ids):
    seg = jnp.full(pos.shape, -1, jnp.int32)
    for b, name in enumerate(ids):
        seg = jnp.where(pos // SPAN == b + 1, name, seg)
    return seg


def segment_masks(rows, ids):
    ri, ci = iota2((rows, rows), 0), iota2((rows, rows), 1)
    same = segment_of(ri, ids) == segment_of(ci, ids)
    return same, ri, ci


def exact_pieces(x):
    one = x.astype(BF16).astype(F32)
    two = (x - one).astype(BF16).astype(F32)
    three = x - one - two
    return jnp.concatenate([one, two, three, jnp.zeros_like(x)], axis=0).astype(BF16)


def exact_rows_dot(x, mask):
    parts = dot_nn(exact_pieces(x), mask)
    return parts[0:8] + (parts[8:16] + parts[16:24])


def col(cols, lane):
    return cols[:, lane : lane + 1]


def prefix_kernel(br_ref, q_ref, k_ref, v_ref, w_ref, d_ref, rows_ref, cols_ref, state_ref):
    rows = q_ref.shape[0]
    heads = w_ref.shape[0]
    key_heads = q_ref.shape[1] // DK
    rep = heads // key_heads
    blocks = rows // SPAN - 1
    ids = response_ids(br_ref, blocks)
    same, ri, ci = segment_masks(rows, ids)
    upto = (same & (ri <= ci)).astype(F32).astype(BF16)
    pad = jnp.zeros((8 - heads, rows), F32)
    g8 = exact_rows_dot(jnp.concatenate([d_ref[...], pad], axis=0), upto)
    b8 = jnp.concatenate([w_ref[...], pad], axis=0)
    lane = iota2((rows, 128), 1)
    norms = jnp.zeros((rows, 128), F32)
    for kh in range(key_heads):
        kf = k_ref[:, kh * DK : (kh + 1) * DK].astype(F32)
        qf = q_ref[:, kh * DK : (kh + 1) * DK].astype(F32)
        rk = lax.rsqrt(jnp.sum(kf * kf, axis=1, keepdims=True) + EPS)
        rq = lax.rsqrt(jnp.sum(qf * qf, axis=1, keepdims=True) + EPS) * (DK**-0.5)
        norms = jnp.where(lane == ROW_RK + kh, rk, norms)
        norms = jnp.where(lane == ROW_RQ + kh, rq, norms)
    norms_t = norms.T
    rows_ref[...] = jnp.concatenate([g8, b8, norms_t[ROW_RK:ROW_END]], axis=0)
    first = jnp.concatenate([g8, b8, jnp.zeros((112, rows), F32)], axis=0)
    cols = first.T + norms
    cols_ref[...] = cols

    n = rep * SPAN
    pi, pj = iota2((n, n), 0), iota2((n, n), 1)
    strict = (pi > pj) & (pi // SPAN == pj // SPAN)
    for kh in range(key_heads):
        kp = k_ref[0:SPAN, kh * DK : (kh + 1) * DK]
        k2 = jnp.concatenate([kp] * rep, axis=0)

        def stack(base, each):
            return jnp.concatenate(
                [cols[0:SPAN, base + (kh * rep + r if each else kh) :][:, 0:1] for r in range(rep)],
                axis=0,
            )

        g2 = stack(ROW_G, True)
        b2 = stack(ROW_B, True)
        rk2 = stack(ROW_RK, False)
        last = jnp.concatenate(
            [jnp.broadcast_to(g2[(r + 1) * SPAN - 1 : (r + 1) * SPAN], (SPAN, 1)) for r in range(rep)],
            axis=0,
        )
        gm = jnp.broadcast_to(g2, (n, n))
        rm = jnp.broadcast_to(rk2, (n, n))
        decay = jnp.exp(jnp.where(strict, gm - gm.T, -1e30))
        lower = dot_nt(k2, k2) * (rm * rm.T) * (b2 * decay)
        inv = unit_lower_inverse(lower, SPAN)
        v2 = jnp.concatenate(
            [v_ref[:, (kh * rep + r) * DV : (kh * rep + r + 1) * DV] for r in range(rep)], axis=0
        ).astype(F32)
        u2 = dot3(inv, b2 * v2)
        weighted = u2 * (jnp.exp(last - g2) * rk2)
        wh, wl = halves(weighted)
        for r in range(rep):
            cut = slice(r * SPAN, (r + 1) * SPAN)
            state_ref[kh * rep + r] = (dot_tn(kp, wh[cut]) + dot_tn(kp, wl[cut])).astype(BF16)


def system_kernel(br_ref, q_ref, k_ref, rows_ref, cols_ref, n_ref, nt_ref, m_ref, mt_ref):
    rows = q_ref.shape[0]
    rep = n_ref.shape[0]
    kh = pl.program_id(0)
    ids = response_ids(br_ref, rows // SPAN - 1)
    same, ri, ci = segment_masks(rows, ids)
    causal = same & (ri >= ci)
    causal_t = same & (ri <= ci)
    strict = same & (ri > ci)
    q, k = q_ref[...], k_ref[...]
    lane = iota2((rows, 128), 1)
    cols = cols_ref[...]

    def pick(base):
        return jnp.sum(jnp.where(lane == base, cols, 0.0), axis=1, keepdims=True)

    def pick_row(base):
        return rows_ref[pl.ds(base, 1), :]

    rk_c, rq_c = pick(ROW_RK + kh), pick(ROW_RQ + kh)
    rk_r, rq_r = pick_row(ROW_RK + kh), pick_row(ROW_RQ + kh)
    kk = dot_nt(k, k) * (rk_c * rk_r)
    qk = dot_nt(q, k) * (rq_c * rk_r)
    kq = dot_nt(k, q) * (rk_c * rq_r)
    half = rows // 2
    for r in range(rep):
        h = kh * rep + r
        g_c, b_c = pick(ROW_G + h), pick(ROW_B + h)
        g_r = pick_row(ROW_G + h)
        diff = g_c - g_r
        decay = jnp.exp(jnp.where(causal, diff, -1e30))
        decay_t = jnp.exp(jnp.where(causal_t, -diff, -1e30))
        m_ref[r] = (qk * decay).astype(BF16)
        mt_ref[r] = (kq * decay_t).astype(BF16)
        lower = jnp.where(strict, kk * (b_c * decay), 0.0)
        t11 = unit_lower_inverse(lower[:half, :half], half)
        t22 = unit_lower_inverse(lower[half:, half:], half)
        t21 = -dot3(t22, dot3(lower[half:, :half], t11))
        eye = (iota2((half, half), 0) == iota2((half, half), 1)).astype(F32)
        zero = jnp.zeros((half, half), F32)
        n_ref[r, :half, :half] = (t11 - eye).astype(BF16)
        n_ref[r, :half, half:] = zero.astype(BF16)
        n_ref[r, half:, :half] = t21.astype(BF16)
        n_ref[r, half:, half:] = (t22 - eye).astype(BF16)
        nt_ref[r, :half, :half] = (t11 - eye).T.astype(BF16)
        nt_ref[r, half:, :half] = zero.astype(BF16)
        nt_ref[r, :half, half:] = t21.T.astype(BF16)
        nt_ref[r, half:, half:] = (t22 - eye).T.astype(BF16)


def forward_kernel(
    br_ref, po_ref, q_ref, k_ref, v_ref, z_ref, cols_ref, n_ref, m_ref, st_ref,
    normed_ref, o_ref, u_ref, r_ref, y_ref,
):
    rows = q_ref.shape[0]
    h = pl.program_id(0)
    blocks = rows // SPAN - 1
    ids = response_ids(br_ref, blocks)
    lane = iota2((rows, 128), 1)
    cols = cols_ref[...]

    def pick(base):
        return jnp.sum(jnp.where(lane == base, cols, 0.0), axis=1, keepdims=True)

    kh = h // HEAD_REP[0]
    g_c, b_c = pick(ROW_G + h), pick(ROW_B + h)
    rk_c, rq_c = pick(ROW_RK + kh), pick(ROW_RQ + kh)
    growth = jnp.exp(g_c)
    zs, ys = [jnp.zeros((SPAN, DV), F32)], [jnp.zeros((SPAN, DV), F32)]
    for b in range(blocks):
        state = st_ref[po_ref[ids[b] // RESP_PER], 0]
        cut = slice((b + 1) * SPAN, (b + 2) * SPAN)
        zs.append(dot_nn(k_ref[cut, :], state))
        ys.append(dot_nn(q_ref[cut, :], state))
    start_v = jnp.concatenate(zs, axis=0) * (growth * rk_c)
    start_o = jnp.concatenate(ys, axis=0) * (growth * rq_c)
    right = b_c * (v_ref[...].astype(F32) - start_v)
    update = right + dot_nn(n_ref[0], right.astype(BF16))
    update16 = update.astype(BF16)
    out = start_o + dot_nn(m_ref[0], update16)
    inv = lax.rsqrt(jnp.mean(out * out, axis=1, keepdims=True) + EPS)
    gate = z_ref[...].astype(F32)
    normed_ref[...] = (out * inv * (gate / (1.0 + jnp.exp(-gate)))).astype(BF16)
    o_ref[...] = out
    u_ref[0] = update16
    r_ref[0] = right
    y_ref[0] = start_o


def backward_state_kernel(
    br_ref, po_ref, q_ref, k_ref, z_ref, gn_ref, o_ref, cols_ref, nt_ref, mt_ref,
    dz_ref, do_ref, dr_ref, gs_ref,
):
    rows = q_ref.shape[0]
    h = pl.program_id(0)
    kh = h // HEAD_REP[0]
    blocks = rows // SPAN - 1
    ids = response_ids(br_ref, blocks)
    lane = iota2((rows, 128), 1)
    cols = cols_ref[...]

    def pick(base):
        return jnp.sum(jnp.where(lane == base, cols, 0.0), axis=1, keepdims=True)

    g_c, b_c = pick(ROW_G + h), pick(ROW_B + h)
    rk_c, rq_c = pick(ROW_RK + kh), pick(ROW_RQ + kh)
    growth = jnp.exp(g_c)
    out = o_ref[...]
    gate = z_ref[...].astype(F32)
    gn = gn_ref[...]
    inv = lax.rsqrt(jnp.mean(out * out, axis=1, keepdims=True) + EPS)
    sig = 1.0 / (1.0 + jnp.exp(-gate))
    silu = gate * sig
    unit = out * inv
    dz_ref[...] = gn * unit * (sig * (1.0 + gate * (1.0 - sig)))
    dh = gn * silu
    dout = inv * (dh - unit * jnp.mean(dh * unit, axis=1, keepdims=True))
    do_ref[0] = dout
    dupdate = dot_nn(mt_ref[0], dout.astype(BF16))
    dright = dupdate + dot_nn(nt_ref[0], dupdate.astype(BF16))
    dr_ref[0] = dright
    dkey = (dright * (-(b_c * growth * rk_c))).astype(BF16)
    dqry = (dout * (growth * rq_c)).astype(BF16)
    gs_ref[...] = jnp.zeros(gs_ref.shape, BF16)
    parts = []
    owners = [po_ref[ids[b] // RESP_PER] for b in range(blocks)]
    for b in range(blocks):
        cut = slice((b + 1) * SPAN, (b + 2) * SPAN)
        parts.append(dot_tn(k_ref[cut, :], dkey[cut]) + dot_tn(q_ref[cut, :], dqry[cut]))
    for b in range(blocks):
        total = parts[b]
        for c in range(blocks):
            if c != b:
                total = total + jnp.where(owners[c] == owners[b], 1.0, 0.0) * parts[c]
        gs_ref[owners[b], 0] = total.astype(BF16)


def backward_rest_kernel(
    br_ref, po_ref, q_ref, k_ref, v_ref, rows_ref, cols_ref, st_ref, do_ref, dr_ref, u_ref,
    r_ref, y_ref, dq_ref, dk_ref, dv_ref, dw_ref, dd_ref, acc_ref,
):
    rows = q_ref.shape[0]
    rep = u_ref.shape[0]
    heads = dw_ref.shape[0]
    kh = pl.program_id(0)
    blocks = rows // SPAN - 1
    ids = response_ids(br_ref, blocks)
    same, ri, ci = segment_masks(rows, ids)
    causal = same & (ri >= ci)
    causal_t = same & (ri <= ci)
    off_diag = ri != ci
    lane = iota2((rows, 128), 1)
    cols = cols_ref[...]

    def pick(base):
        return jnp.sum(jnp.where(lane == base, cols, 0.0), axis=1, keepdims=True)

    def pick_row(base):
        return rows_ref[pl.ds(base, 1), :]

    @pl.when(kh == 0)
    def _():
        acc_ref[...] = jnp.zeros_like(acc_ref)

    q, k = q_ref[...], k_ref[...]
    rk_c, rq_c = pick(ROW_RK + kh), pick(ROW_RQ + kh)
    rk_r, rq_r = pick_row(ROW_RK + kh), pick_row(ROW_RQ + kh)
    kk = dot_nt(k, k)
    qk = dot_nt(q, k)
    kq = dot_nt(k, q)
    dqh = jnp.zeros((rows, DK), F32)
    dkh = jnp.zeros((rows, DK), F32)
    for r in range(rep):
        h = kh * rep + r
        g_c, b_c = pick(ROW_G + h), pick(ROW_B + h)
        g_r, b_r = pick_row(ROW_G + h), pick_row(ROW_B + h)
        growth = jnp.exp(g_c)
        diff = g_c - g_r
        decay = jnp.exp(jnp.where(causal, diff, -1e30))
        decay_t = jnp.exp(jnp.where(causal_t, -diff, -1e30))
        dout, dright, right, start_o = do_ref[r], dr_ref[r], r_ref[r], y_ref[r]
        u16 = u_ref[r]
        do16, dr16 = dout.astype(BF16), dright.astype(BF16)
        p1 = dot_nt(do16, u16) * (decay * rk_r)
        p1t = dot_nt(u16, do16) * (decay_t * rq_r)
        strict_w = jnp.where(off_diag, decay, 0.0)
        strict_wt = jnp.where(off_diag, decay_t, 0.0)
        p2 = dot_nt(dr16, u16) * (strict_w * (-b_c) * rk_r)
        p2t = dot_nt(u16, dr16) * (strict_wt * (-b_r) * rk_r)
        e2sum = jnp.sum(p2 * kk, axis=1, keepdims=True) * rk_c
        e1sum = jnp.sum(p1 * qk, axis=1, keepdims=True) * rq_c
        tsum = jnp.sum(p1t * kq + p2t * kk, axis=1, keepdims=True) * rk_c
        dqh = dqh + dot_nn(p1.astype(BF16), k)
        dkh = dkh + dot_nn((p2 + p2t).astype(BF16), k) + dot_nn(p1t.astype(BF16), q)
        dkey = (dright * (-(b_c * growth))).astype(BF16)
        dqry = (dout * growth).astype(BF16)
        dks, dqs = [jnp.zeros((SPAN, DK), F32)], [jnp.zeros((SPAN, DK), F32)]
        for b in range(blocks):
            state = st_ref[po_ref[ids[b] // RESP_PER], r]
            cut = slice((b + 1) * SPAN, (b + 2) * SPAN)
            dks.append(dot_nt(dkey[cut], state))
            dqs.append(dot_nt(dqry[cut], state))
        dkh = dkh + jnp.concatenate(dks, axis=0)
        dqh = dqh + jnp.concatenate(dqs, axis=0)
        vf = v_ref[:, r * DV : (r + 1) * DV].astype(F32)
        dr_r = jnp.sum(dright * right, axis=1, keepdims=True)
        dr_v = jnp.sum(dright * vf, axis=1, keepdims=True)
        do_y = jnp.sum(dout * start_o, axis=1, keepdims=True)
        dv_ref[:, r * DV : (r + 1) * DV] = b_c * dright
        db = (e2sum + dr_r) / b_c
        dg = e1sum + e2sum - tsum + do_y + (dr_r - b_c * dr_v)
        acc = acc_ref[...]
        acc = jnp.where(lane == h, dg, acc)
        acc_ref[...] = jnp.where(lane == 8 + h, db, acc)
    kf, qf = k.astype(F32), q.astype(F32)
    dk_ref[...] = rk_c * (dkh - kf * (rk_c * rk_c * jnp.sum(kf * dkh, axis=1, keepdims=True)))
    dq_ref[...] = rq_c * (
        dqh - qf * (rq_c * rq_c * DK * jnp.sum(qf * dqh, axis=1, keepdims=True))
    )

    @pl.when(kh == pl.num_programs(0) - 1)
    def _():
        acc_t = acc_ref[...].T
        tail = causal.astype(F32).astype(BF16)
        dd_ref[...] = exact_rows_dot(acc_t[0:8], tail)[0:heads]
        dw_ref[...] = acc_t[8 : 8 + heads]


def backward_prefix_kernel(
    k_ref, v_ref, rows_ref, cols_ref, nt_ref, u_ref, gs_ref, dk_in, dv_in, dw_in, dd_in,
    dk_ref, dv_ref, dw_ref, dd_ref,
):
    heads = u_ref.shape[0]
    key_heads = k_ref.shape[1] // DK
    rep = heads // key_heads
    n = SPAN
    ri, ci = iota2((n, n), 0), iota2((n, n), 1)
    causal, causal_t, off_diag = ri >= ci, ri <= ci, ri != ci
    cols = cols_ref[...]
    lane = iota2((n, 128), 1)
    acc = jnp.zeros((n, 128), F32)
    last_row = iota2((n, 1), 0) == n - 1
    for kh in range(key_heads):
        k = k_ref[:, kh * DK : (kh + 1) * DK]
        kf = k.astype(F32)
        kk = dot_nt(k, k)
        rk_c = col(cols, ROW_RK + kh)
        rk_r = rows_ref[ROW_RK + kh : ROW_RK + kh + 1, 0:n]
        dkh = jnp.zeros((n, DK), F32)
        for r in range(rep):
            h = kh * rep + r
            g_c, b_c = col(cols, ROW_G + h), col(cols, ROW_B + h)
            g_r = rows_ref[ROW_G + h : ROW_G + h + 1, 0:n]
            b_r = rows_ref[ROW_B + h : ROW_B + h + 1, 0:n]
            diff = g_c - g_r
            decay = jnp.exp(jnp.where(causal & off_diag, diff, -1e30))
            decay_t = jnp.exp(jnp.where(causal_t & off_diag, -diff, -1e30))
            rest = jnp.exp(g_c[n - 1 : n] - g_c)
            sh, sl = halves(gs_ref[h])
            u16 = u_ref[h]
            dupdate = (rest * rk_c) * (dot_nn(k, sh) + dot_nn(k, sl))
            dright = dupdate + dot_nn(nt_ref[h][:, 0:n], dupdate.astype(BF16))
            dr16 = dright.astype(BF16)
            p2 = dot_nt(dr16, u16) * (decay * (-b_c) * rk_r)
            p2t = dot_nt(u16, dr16) * (decay_t * (-b_r) * rk_r)
            e2sum = jnp.sum(p2 * kk, axis=1, keepdims=True) * rk_c
            tsum = jnp.sum(p2t * kk, axis=1, keepdims=True) * rk_c
            back = rest * (dot_nt(u16, sh) + dot_nt(u16, sl))
            dkh = dkh + back + dot_nn((p2 + p2t).astype(BF16), k)
            e3 = rk_c * jnp.sum(kf * back, axis=1, keepdims=True)
            vf = v_ref[:, h * DV : (h + 1) * DV].astype(F32)
            db = e2sum / b_c + jnp.sum(dright * vf, axis=1, keepdims=True)
            dg = e2sum - tsum - e3 + jnp.where(last_row, jnp.sum(e3), 0.0)
            dv_ref[:, h * DV : (h + 1) * DV] = dv_in[:, h * DV : (h + 1) * DV] + b_c * dright
            acc = jnp.where(lane == h, dg, acc)
            acc = jnp.where(lane == 8 + h, db, acc)
        dk_ref[:, kh * DK : (kh + 1) * DK] = dk_in[:, kh * DK : (kh + 1) * DK] + rk_c * (
            dkh - kf * (rk_c * rk_c * jnp.sum(kf * dkh, axis=1, keepdims=True))
        )
    acc_t = jnp.concatenate([acc, jnp.zeros((128 - n, 128), F32)], axis=0).T
    si, sj = iota2((128, 128), 0), iota2((128, 128), 1)
    tail = ((si >= sj) & (si < n)).astype(F32).astype(BF16)
    dd_ref[...] = dd_in[...] + exact_rows_dot(acc_t[0:8], tail)[0:heads]
    dw_ref[...] = dw_in[...] + acc_t[8 : 8 + heads]


HEAD_REP = [2]


def swap(x, bit, axis, size):
    return lax.ppermute(x, axis, [(i, i ^ bit) for i in range(size)])


def shift(x, by, axis, size):
    return lax.ppermute(x, axis, [(i, (i + by) % size) for i in range(size)])


def gather_states(x, size):
    if size > 8:
        return lax.all_gather(x, "seq", axis=0)
    me = lax.axis_index("seq")
    out = jnp.zeros((size,) + x.shape, x.dtype)
    out = lax.dynamic_update_index_in_dim(out, x, me, 0)
    for bit in range(1, size):
        out = lax.dynamic_update_index_in_dim(out, swap(x, bit, "seq", size), me ^ bit, 0)
    return out


def gather_heads(x, size):
    me = lax.axis_index("head")
    out = jnp.zeros((size,) + x.shape, x.dtype)
    out = lax.dynamic_update_index_in_dim(out, x, me, 0)
    for by in range(1, size):
        out = lax.dynamic_update_index_in_dim(
            out, shift(x, by, "head", size), (me - by) % size, 0
        )
    return out


def scatter_heads(parts, size):
    me = lax.axis_index("head")
    total = lax.dynamic_index_in_dim(parts, me, 0, False).astype(F32)
    for by in range(1, size):
        part = lax.dynamic_index_in_dim(parts, (me + by) % size, 0, False)
        total = total + shift(part, by, "head", size).astype(F32)
    return total


def take_half(v, axis, which):
    return lax.dynamic_index_in_dim(v, which, axis, False)


def fold(v, axis, bit, dist, size):
    mine = take_half(v, axis, bit).astype(F32)
    return mine + swap(take_half(v, axis, 1 - bit), dist, "seq", size).astype(F32)


def scatter_seq(x, size):
    if size != 8:
        return lax.psum_scatter(x, "seq", scatter_dimension=0, tiled=False).astype(F32)
    me = lax.axis_index("seq")
    c, xb, yb = me & 1, (me >> 1) & 1, (me >> 2) & 1
    v = x.reshape((2, 2, 2) + x.shape[1:])
    a = fold(v, 2, c, 1, size).astype(x.dtype)
    half = a.shape[2] // 2
    first = fold(a[:, :, :half], 1, xb, 2, size).astype(x.dtype)
    second = fold(a[:, :, half:], 0, yb, 4, size).astype(x.dtype)
    first = fold(first, 0, yb, 4, size)
    second = fold(second, 0, xb, 2, size)
    return jnp.concatenate([first, second], axis=0)


def per_device(
    n_seq, n_head, query, key, value, gate, write, decay, weight, cotangent, br, po
):
    rows = query.shape[0]
    heads = write.shape[0]
    key_heads = query.shape[1] // DK
    rep = heads // key_heads
    HEAD_REP[0] = rep
    sds = jax.ShapeDtypeStruct
    width = weight.shape[0]
    cut = width // n_head

    cot = gather_heads(cotangent, n_head)
    weight4 = weight.reshape(n_head, cut, weight.shape[1])

    def whole(*shape):
        return pl.BlockSpec(shape, lambda *_: (0,) * len(shape))

    def call(body, prefetch, grid, ins, outs, shapes, args, scratch=(), aliases=None, flops=10**8):
        return pl.pallas_call(
            body,
            grid_spec=pltpu.PrefetchScalarGridSpec(
                num_scalar_prefetch=prefetch, grid=grid, in_specs=ins, out_specs=outs,
                scratch_shapes=list(scratch),
            ),
            out_shape=shapes,
            input_output_aliases=aliases or {},
            cost_estimate=pl.CostEstimate(flops=flops, transcendentals=0, bytes_accessed=10**6),
            name=body.__name__,
        )(*args)

    rows_tab, cols_tab, state = call(
        prefix_kernel, 1, (1,),
        [whole(rows, key_heads * DK), whole(rows, key_heads * DK), whole(SPAN, heads * DV),
         whole(heads, rows), whole(heads, rows)],
        [whole(ROW_END, rows), whole(rows, 128), whole(heads, DK, DV)],
        [sds((ROW_END, rows), F32), sds((rows, 128), F32), sds((heads, DK, DV), BF16)],
        (br, query, key, value, write, decay),
    )
    states = gather_states(state, n_seq)

    by_key = pl.BlockSpec((rows, DK), lambda h, *_: (0, h))
    square = pl.BlockSpec((rep, rows, rows), lambda h, *_: (h, 0, 0))
    tables = [whole(ROW_END, rows), whole(rows, 128)]
    nmat, nmat_t, mmat, mmat_t = call(
        system_kernel, 1, (key_heads,), [by_key, by_key] + tables, [square] * 4,
        [sds((heads, rows, rows), BF16)] * 4, (br, query, key, rows_tab, cols_tab),
    )

    key_of = pl.BlockSpec((rows, DK), lambda h, *_: (0, h // rep))
    by_head = pl.BlockSpec((rows, DV), lambda h, *_: (0, h))
    square1 = pl.BlockSpec((1, rows, rows), lambda h, *_: (h, 0, 0))
    rows1 = pl.BlockSpec((1, rows, DV), lambda h, *_: (h, 0, 0))
    states1 = pl.BlockSpec((n_seq, 1, DK, DV), lambda h, *_: (0, h, 0, 0))
    per_head32 = sds((heads, rows, DV), F32)
    flat32 = sds((rows, heads * DV), F32)
    normed, outs, update, right, start_o = call(
        forward_kernel, 2, (heads,),
        [key_of, key_of, by_head, by_head, whole(rows, 128), square1, square1, states1],
        [by_head, by_head, rows1, rows1, rows1],
        [sds((rows, heads * DV), BF16), flat32, sds((heads, rows, DV), BF16), per_head32, per_head32],
        (br, po, query, key, value, gate, cols_tab, nmat, mmat, states),
    )

    grad_normed = jnp.einsum("jrd,jdv->rv", cot, weight4, preferred_element_type=F32)
    grad_weight = scatter_seq(
        jnp.einsum("jrd,rv->jdv", cot, normed, preferred_element_type=F32)
        .astype(BF16)
        .reshape(n_seq, width // n_seq, -1),
        n_seq,
    )
    layer_out = scatter_heads(
        jnp.einsum("rv,jdv->jrd", normed, weight4, preferred_element_type=F32).astype(BF16), n_head
    ).astype(BF16)

    grad_gate, dout, dright, gs = call(
        backward_state_kernel, 2, (heads,),
        [key_of, key_of, by_head, by_head, by_head, whole(rows, 128), square1, square1],
        [by_head, rows1, rows1, states1],
        [flat32, per_head32, per_head32, sds((n_seq, heads, DK, DV), BF16)],
        (br, po, query, key, gate, grad_normed, outs, cols_tab, nmat_t, mmat_t),
    )
    own = scatter_seq(gs.reshape(n_seq, heads * DK, DV), n_seq).reshape(heads, DK, DV)

    wide_v = pl.BlockSpec((rows, rep * DV), lambda h, *_: (0, h))
    rows_rep = pl.BlockSpec((rep, rows, DV), lambda h, *_: (h, 0, 0))
    states_rep = pl.BlockSpec((n_seq, rep, DK, DV), lambda h, *_: (0, h, 0, 0))
    keys32 = sds((rows, key_heads * DK), F32)
    small32 = sds((heads, rows), F32)
    dq, dk, dv, dw, dd = call(
        backward_rest_kernel, 2, (key_heads,),
        [by_key, by_key, wide_v] + tables + [states_rep] + [rows_rep] * 5,
        [by_key, by_key, wide_v, whole(heads, rows), whole(heads, rows)],
        [keys32, keys32, flat32, small32, small32],
        (br, po, query, key, value, rows_tab, cols_tab, states, dout, dright, update, right, start_o),
        scratch=[pltpu.VMEM((rows, 128), F32)],
    )
    dk, dv, dw, dd = call(
        backward_prefix_kernel, 0, (1,),
        [whole(SPAN, key_heads * DK), whole(SPAN, heads * DV), whole(ROW_END, 128),
         whole(SPAN, 128), whole(heads, SPAN, 128), whole(heads, SPAN, DV), whole(heads, DK, DV),
         whole(SPAN, key_heads * DK), whole(SPAN, heads * DV), whole(heads, 128), whole(heads, 128)],
        [whole(SPAN, key_heads * DK), whole(SPAN, heads * DV), whole(heads, 128), whole(heads, 128)],
        [keys32, flat32, small32, small32],
        (key, value, rows_tab, cols_tab, nmat_t, update, own, dk, dv, dw, dd),
        aliases={7: 0, 8: 1, 9: 2, 10: 3},
    )
    return layer_out, dq, dk, dv, grad_gate, dw, dd, grad_weight


def solution(mesh):
    n_seq, n_head = mesh.shape["seq"], mesh.shape["head"]
    both, turned = P("seq", "head"), P("head", "seq")
    return jax.shard_map(
        partial(per_device, n_seq, n_head),
        mesh=mesh,
        in_specs=(both, both, both, both, turned, turned, P(None, "head"), both, P(), P()),
        out_specs=(both, both, both, both, both, turned, turned, both),
        check_vma=False,
    )
```

time: 394 us -> 141 us (0.36)
  other arithmetic: 147 us -> 7.63 us
  matrix products: 131 us -> 5.13 us
  Pallas kernels: 0 us -> 48 us
  local copies, waits for them, and re-layouts: 67.9 us -> 22.9 us
  starting transfers between devices: 5.87 us -> 30.6 us
  loops' own time: 17.6 us -> 0 us
  waiting for transfers between devices: 8.62 us -> 25.1 us
  between operations: 15.4 us -> 1.14 us
    dot_general x74 -> x3, matrix products: 123 us -> 5.13 us  [the longest x1 2.74 us: per_device(): jnp.einsum('jrd,jdv->rv', cot, weight4, preferred_element_type=F32)]
    another operation x10 -> x0, other arithmetic: 86.3 us -> none  [the longest x4 80.1 us: span_parts(): lax.linalg.triangular_solve(system, right_side, left_side=True, lower=Tru...]
    pallas_call x0 -> x6, Pallas kernels: none -> 48 us  [call(): pl.pallas_call(body, grid_spec=pltpu.PrefetchScalarGridSpec(num_scalar_pr...]
    ppermute x0 -> x23, starting transfers between devices: none -> 30.6 us  [the longest x17 17.1 us: swap(): return lax.ppermute(x, axis, [(i, i ^ bit) for i in range(size)])]
    ppermute x0 -> x23, waiting for transfers between devices: none -> 25.1 us  [the longest x6 12.7 us: shift(): return lax.ppermute(x, axis, [(i, (i + by) % size) for i in range(size)])]
    reduce_sum x23 -> x0, other arithmetic: 20.2 us -> none  [the longest x4 4.66 us: span_apply(): growth[..., None]]
    another operation x2 -> x0, loops' own time: 17.6 us -> none  [respond_blocks(): lax.scan(respond_advance, carry_in, (span_terms, block_flags, owners))]
    dynamic_slice x12 -> x0, local copies, waits for them, and re-layouts: 15.1 us -> none  [respond_blocks(): lax.scan(respond_advance, carry_in, (span_terms, block_flags, owners))]
  transfers between devices with their start and end apart: 5 -> 23, of which waited for: 2 -> 7; matrix products, arithmetic and copies ran while one was open for 51% -> 15% of each run, Pallas kernels for 0% -> 25%
where the time goes in v1:
time: 141 us
  Pallas kernels  48 us (34%)
  starting transfers between devices  30.6 us (22%)
  waiting for transfers between devices  25.1 us (18%)
  local copies, waits for them, and re-layouts  22.9 us (16%)
  other arithmetic  7.63 us (5%)
  matrix products  5.13 us (4%)
    pallas_call x6, Pallas kernels, call(): pl.pallas_call(body, grid_spec=pltpu.PrefetchScalarGridSpec(num_scalar_pr...  48 us
    ppermute x17, starting transfers between devices, swap(): return lax.ppermute(x, axis, [(i, i ^ bit) for i in range(size)])  17.1 us
    ppermute x6, starting transfers between devices, shift(): return lax.ppermute(x, axis, [(i, (i + by) % size) for i in range(size)])  13.5 us
    ppermute x6, waiting for transfers between devices, shift(): return lax.ppermute(x, axis, [(i, (i + by) % size) for i in range(size)])  12.7 us
    ppermute x17, waiting for transfers between devices, swap(): return lax.ppermute(x, axis, [(i, i ^ bit) for i in range(size)])  12.5 us
    broadcast_in_dim x3, local copies, waits for them, and re-layouts, gather_heads(): lax.dynamic_update_index_in_dim(out, shift(x, by, 'head', size), (me - by...  4.66 us
    dynamic_update_slice x7, local copies, waits for them, and re-layouts, gather_states(): lax.dynamic_update_index_in_dim(out, swap(x, bit, 'seq', size), me ^ bit, 0)  4.66 us
    dynamic_update_slice x3, local copies, waits for them, and re-layouts, gather_heads(): lax.dynamic_update_index_in_dim(out, shift(x, by, 'head', size), (me - by...  4.07 us
  transfers between devices with their start and end apart: 23, of which 7 were waited for; matrix products, arithmetic and copies ran while one was open for 15% of the time, Pallas kernels for 25%

profile of v1, /device:TPU:0, one launch (start us, length us, event | category | flops | bytes accessed | tf_op | source)
XLA Modules:
  0.0 140.6 jit_solution(2892647228513490766)
XLA Ops:
  0.6 7.0 %prefix_kernel.1 = (f32[32,256]{1,0:T(8,128)}, f32[256,128]{1,0:T(8,128)}, bf16[4,128,128]{2,1,0:T(8,128)(2,1)}) custom-call(s32[24]{0:T(128)} %br_ref.9, bf16[256,256]{1,0:T(8,128)(2,1)} %q_ref.9, bf16[256,256]{1,0:T(8,128)(2,1)} %k_ref.11, bf16[256,512]{1,0:T(8,128)(2,1)} %v_ref.7, f32[4,256]{1,0:T(4,128)} %w_ref.1, f32[4,256]{1,0:T(4,128)} %d_ref.1), custom_call_target="tpu_custom_call" | custom-call | flops 100000000 | bytes 1000000 | tf_op jit(solution)/shard_map/prefix_kernel/pallas_call | solution.py:531
  8.1 2.5 %collective-permute-start.1 = (bf16[4,128,128]{2,1,0:T(8,128)(2,1)}, bf16[4,128,128]{2,1,0:T(8,128)(2,1)}, u32[]{:S(2)}, u32[]{:S(2)}) collective-permute-start(bf16[4,128,128]{2,1,0:T(8,128)(2,1)} %get-tuple-element.37), channel_id=1, source_target_pairs={{0,8},{4,12},{8,0},{12,4},{16,24},{20,28},{24,16},{28,20},{1,9},{5... | collective-permute-start | bytes 393224 | tf_op jit(solution)/shard_map/ppermute | solution.py:450
  10.7 1.8 %collective-permute-start.3 = (bf16[4,128,128]{2,1,0:T(8,128)(2,1)}, bf16[4,128,128]{2,1,0:T(8,128)(2,1)}, u32[]{:S(2)}, u32[]{:S(2)}) collective-permute-start(bf16[4,128,128]{2,1,0:T(8,128)(2,1)} %get-tuple-element.37), channel_id=1, source_target_pairs={{0,16},{4,20},{8,24},{12,28},{16,0},{20,4},{24,8},{28,12},{1,17},{... | collective-permute-start | bytes 393224 | tf_op jit(solution)/shard_map/ppermute | solution.py:450
  14.8 18.5 %system_kernel.1 = (bf16[4,256,256]{2,1,0:T(8,128)(2,1)}, bf16[4,256,256]{2,1,0:T(8,128)(2,1)}, bf16[4,256,256]{2,1,0:T(8,128)(2,1)}, bf16[4,256,256]{2,1,0:T(8,128)(2,1)}) custom-call(s32[24]{0:T(128)} %br_ref.9, bf16[256,256]{1,0:T(8,128)(2,1)} %q_ref.9, bf16[256,256]{1,0:T(8,128)(2,1)} %k_ref.11, f32[32,256]{1,0:T(8,128)} %get-tuple-element.34.rows_ref, ...), custom_call_target="tpu_custom_call" | custom-call | flops 100000000 | bytes 1000000 | tf_op jit(solution)/shard_map/system_kernel/pallas_call | solution.py:531
  33.5 2.6 %collective-permute-start.5 = (bf16[4,128,128]{2,1,0:T(8,128)(2,1)S(1)}, bf16[4,128,128]{2,1,0:T(8,128)(2,1)S(1)}, u32[]{:S(2)}, u32[]{:S(2)}) collective-permute-start(bf16[4,128,128]{2,1,0:T(8,128)(2,1)S(1)} %copy-done.8), channel_id=1, source_target_pairs={{0,24},{4,28},{8,16},{12,20},{16,8},{20,12},{24,0},{28,4},{1,25},{... | collective-permute-start | bytes 393224 | tf_op jit(solution)/shard_map/ppermute | solution.py:450
  38.3 1.7 %collective-permute-start.10 = (bf16[256,512]{1,0:T(8,128)(2,1)}, bf16[256,512]{1,0:T(8,128)(2,1)S(1)}, u32[]{:S(2)}, u32[]{:S(2)}) collective-permute-start(bf16[256,512]{1,0:T(8,128)(2,1)} %param.17), channel_id=1, source_target_pairs={{0,1},{1,2},{2,3},{3,0},{4,5},{5,6},{6,7},{7,4},{8,9},{9,10},{10,1... | collective-permute-start | bytes 786440 | tf_op jit(solution)/shard_map/ppermute | solution.py:454
  41.0 2.7 %collective-permute-start.11 = (bf16[256,512]{1,0:T(8,128)(2,1)}, bf16[256,512]{1,0:T(8,128)(2,1)}, u32[]{:S(2)}, u32[]{:S(2)}) collective-permute-start(bf16[256,512]{1,0:T(8,128)(2,1)} %param.17), channel_id=1, source_target_pairs={{0,2},{1,3},{2,0},{3,1},{4,6},{5,7},{6,4},{7,5},{8,10},{9,11},{10,... | collective-permute-start | bytes 786440 | tf_op jit(solution)/shard_map/ppermute | solution.py:454
  44.6 1.4 collective-permute-start.12
  48.0 6.1 %forward_kernel.1 = (bf16[256,512]{1,0:T(8,128)(2,1)}, f32[256,512]{1,0:T(8,128)}, bf16[4,256,128]{2,1,0:T(8,128)(2,1)}, f32[4,256,128]{2,1,0:T(8,128)}, f32[4,256,128]{2,1,0:T(8,128)}) custom-call(s32[24]{0:T(128)} %br_ref.9, s32[8]{0:T(128)} %po_ref.5, bf16[256,256]{1,0:T(8,128)(2,1)} %q_ref.9, bf16[256,256]{1,0:T(8,128)(2,1)} %k_ref.11, ...), custom_call_target="tpu_custom_call" | custom-call | flops 100000000 | bytes 1000000 | tf_op jit(solution)/shard_map/forward_kernel/pallas_call | solution.py:531
  54.1 1.7 %convolution_convert_fusion.1 = bf16[256,4,512]{2,0,1:T(8,128)(2,1)S(1)} fusion(bf16[4,512,512]{2,1,0:T(8,128)(2,1)S(1)} %bitcast.98, bf16[256,512]{1,0:T(8,128)(2,1)} %get-tuple-element.38), kind=kOutput, calls=%fused_computation.3 | convolution fusion | flops 537395200 | bytes 3407872 | tf_op jit(solution)/shard_map/rv,jdv->jrd/dot_general | solution.py:584
  57.6 2.9 %collective-permute-done.11 = bf16[256,512]{1,0:T(8,128)(2,1)} collective-permute-done((bf16[256,512]{1,0:T(8,128)(2,1)}, bf16[256,512]{1,0:T(8,128)(2,1)}, u32[]{:S(2)}, u32[]{:S(2)}) %collective-permute-start.11) | collective-permute-done | bytes 262176 | tf_op jit(solution)/shard_map/ppermute | solution.py:454
  60.4 1.8 %copy.24 = bf16[1,256,512]{1,2,0:T(8,128)(2,1)} copy(bf16[1,256,512]{2,1,0:T(8,128)(2,1)} %bitcast.16) | data formatting | bytes 524288 | tf_op jit(solution)/shard_map/jit(dynamic_update_index_in_dim)/broadcast_in_dim | solution.py:473
  62.2 1.8 %copy.25 = bf16[1,256,512]{1,2,0:T(8,128)(2,1)} copy(bf16[1,256,512]{2,1,0:T(8,128)(2,1)} %bitcast.17) | data formatting | bytes 524288 | tf_op jit(solution)/shard_map/jit(dynamic_update_index_in_dim)/broadcast_in_dim | solution.py:473
  64.7 1.7 %constant_dynamic-update-slice_fusion.1 = bf16[4,256,512]{1,2,0:T(8,128)(2,1)} fusion(bf16[4,256,512]{1,2,0:T(8,128)(2,1)} %constant_dynamic-update-slice_fusion.2, bf16[1,256,512]{1,2,0:T(8,128)(2,1)} %copy.24, s32[]{:T(128)S(6)} %select_n.134), kind=kLoop, calls=%fused_computation.49 | loop fusion | bytes 524292 | tf_op jit(solution)/shard_map/jit(dynamic_update_index_in_dim)/dynamic_update_slice | solution.py:473
  66.4 1.7 %constant_dynamic-update-slice_fusion = bf16[4,256,512]{1,2,0:T(8,128)(2,1)} fusion(bf16[4,256,512]{1,2,0:T(8,128)(2,1)} %constant_dynamic-update-slice_fusion.1, bf16[1,256,512]{1,2,0:T(8,128)(2,1)} %copy.25, s32[]{:T(128)S(6)} %select_n.136), kind=kLoop, calls=%fused_computation.48 | loop fusion | bytes 524292 | tf_op jit(solution)/shard_map/jit(dynamic_update_index_in_dim)/dynamic_update_slice | solution.py:473
  68.1 2.7 %convolution_bitcast_fusion.gn_ref = f32[256,512]{1,0:T(8,128)} fusion(bf16[4,256,512]{1,2,0:T(8,128)(2,1)} %constant_dynamic-update-slice_fusion, bf16[4,512,512]{2,1,0:T(8,128)(2,1)S(1)} %bitcast.99), kind=kOutput, calls=%fused_computation.4 | convolution fusion | flops 536870912 | bytes 3670016 | tf_op jit(solution)/shard_map/jrd,jdv->rv/dot_general | solution.py:576
  70.8 6.4 %backward_state_kernel.1 = (f32[256,512]{1,0:T(8,128)}, f32[4,256,128]{2,1,0:T(8,128)}, f32[4,256,128]{2,1,0:T(8,128)}, bf16[8,4,128,128]{3,2,1,0:T(8,128)(2,1)}) custom-call(s32[24]{0:T(128)} %br_ref.9, s32[8]{0:T(128)} %po_ref.5, bf16[256,256]{1,0:T(8,128)(2,1)} %q_ref.9, bf16[256,256]{1,0:T(8,128)(2,1)} %k_ref.11, bf16[256,512]{1,0:T(8,128)(2,1)} %z_ref.3, ...), custom_call_target="tpu_custom_call" | custom-call | flops 100000000 | bytes 1000000 | tf_op jit(solution)/shard_map/backward_state_kernel/pallas_call | solution.py:531
  77.3 2.0 %dynamic-slice_bitcast_fusion.1 = bf16[2,2,512,128]{3,2,1,0:T(8,128)(2,1)} fusion(bf16[2,2,2,512,128]{4,3,2,1,0:T(8,128)(2,1)} %bitcast.103, s32[]{:T(128)S(6)} %select_n.138), kind=kLoop, calls=%fused_computation.17 | loop fusion | bytes 1048580 | tf_op jit(solution)/shard_map/jit(dynamic_index_in_dim)/squeeze | solution.py:489
  80.2 7.2 %collective-permute-start.9 = (bf16[256,512]{1,0:T(8,128)(2,1)}, bf16[256,512]{1,0:T(8,128)(2,1)}, u32[]{:S(2)}, u32[]{:S(2)}) collective-permute-start(bf16[256,512]{1,0:T(8,128)(2,1)} %get-tuple-element.61), channel_id=1, source_target_pairs={{0,3},{1,0},{2,1},{3,2},{4,7},{5,4},{6,5},{7,6},{8,11},{9,8},{10,9... | collective-permute-start | bytes 786440 | tf_op jit(solution)/shard_map/ppermute | solution.py:454
  88.6 1.3 copy-done.2
  91.0 6.0 %backward_rest_kernel.1 = (f32[256,256]{1,0:T(8,128)}, f32[256,256]{1,0:T(8,128)}, f32[256,512]{1,0:T(8,128)}, f32[4,256]{1,0:T(4,128)}, f32[4,256]{1,0:T(4,128)}) custom-call(s32[24]{0:T(128)} %br_ref.9, s32[8]{0:T(128)} %po_ref.5, bf16[256,256]{1,0:T(8,128)(2,1)} %q_ref.9, bf16[256,256]{1,0:T(8,128)(2,1)} %k_ref.11, bf16[256,512]{1,0:T(8,128)(2,1)} %v_ref.7, ...), custom_call_target="tpu_custom_call" | custom-call | flops 100000000 | bytes 1000000 | tf_op jit(solution)/shard_map/backward_rest_kernel/pallas_call | solution.py:531
  98.5 1.6 %collective-permute-start.16 = (bf16[2,256,128]{2,1,0:T(8,128)(2,1)S(1)}, bf16[2,256,128]{2,1,0:T(8,128)(2,1)S(1)}, u32[]{:S(2)}, u32[]{:S(2)}) collective-permute-start(bf16[2,256,128]{2,1,0:T(8,128)(2,1)S(1)} %dynamic-slice_bitcast_fusion.9), channel_id=1, source_target_pairs={{0,16},{4,20},{8,24},{12,28},{16,0},{20,4},{24,8},{28,12},{1,17},{... | collective-permute-start | bytes 393224 | tf_op jit(solution)/shard_map/ppermute | solution.py:450
  100.0 9.8 %collective-permute-done.8 = bf16[256,512]{1,0:T(8,128)(2,1)} collective-permute-done((bf16[256,512]{1,0:T(8,128)(2,1)}, bf16[256,512]{1,0:T(8,128)(2,1)}, u32[]{:S(2)}, u32[]{:S(2)}) %collective-permute-start.8) | collective-permute-done | bytes 262176 | tf_op jit(solution)/shard_map/ppermute | solution.py:454
  109.8 1.9 %fusion.6 = bf16[256,512]{1,0:T(8,128)(2,1)} fusion(bf16[256,512]{1,0:T(8,128)(2,1)} %collective-permute-done.9, bf16[256,512]{1,0:T(8,128)(2,1)} %collective-permute-done.8, bf16[256,512]{1,0:T(8,128)(2,1)} %collective-permute-done.7, bf16[256,4,512]{2,0,1:T(8,128)(2,1)S(1)} %convolution_convert_fusion.1, s32[]{:T(128)S(6)} %select_n.124), kind=kLoop, calls=%fused_computation.16 | loop fusion | flops 1048576 | bytes 1310724 | tf_op jit(solution)/shard_map/convert_element_type | solution.py:585
  111.8 1.6 %collective-permute-start.14 = (bf16[2,256,128]{2,1,0:T(8,128)(2,1)S(1)}, bf16[2,256,128]{2,1,0:T(8,128)(2,1)S(1)}, u32[]{:S(2)}, u32[]{:S(2)}) collective-permute-start(bf16[2,256,128]{2,1,0:T(8,128)(2,1)S(1)} %dynamic-slice_bitcast_fusion.10), channel_id=1, source_target_pairs={{0,8},{4,12},{8,0},{12,4},{16,24},{20,28},{24,16},{28,20},{1,9},{5... | collective-permute-start | bytes 393224 | tf_op jit(solution)/shard_map/ppermute | solution.py:450
  114.0 3.6 %collective-permute-done.14 = bf16[2,256,128]{2,1,0:T(8,128)(2,1)S(1)} collective-permute-done((bf16[2,256,128]{2,1,0:T(8,128)(2,1)S(1)}, bf16[2,256,128]{2,1,0:T(8,128)(2,1)S(1)}, u32[]{:S(2)}, u32[]{:S(2)}) %collective-permute-start.14) | collective-permute-done | bytes 131104 | tf_op jit(solution)/shard_map/ppermute | solution.py:450
  117.7 1.6 %collective-permute-start.15 = (bf16[256,128]{1,0:T(8,128)(2,1)S(1)}, bf16[256,128]{1,0:T(8,128)(2,1)S(1)}, u32[]{:S(2)}, u32[]{:S(2)}) collective-permute-start(bf16[256,128]{1,0:T(8,128)(2,1)S(1)} %dynamic-slice_bitcast_fusion.12), channel_id=1, source_target_pairs={{0,16},{4,20},{8,24},{12,28},{16,0},{20,4},{24,8},{28,12},{1,17},{... | collective-permute-start | bytes 196616 | tf_op jit(solution)/shard_map/ppermute | solution.py:450
  119.3 1.5 %fusion = bf16[2,2,256,512]{3,2,1,0:T(8,128)(2,1)S(1)} fusion(bf16[2,2,256,512]{3,2,1,0:T(8,128)(2,1)} %collective-permute-done.18, bf16[2,2,2,256,512]{4,3,2,1,0:T(8,128)(2,1)S(1)} %bitcast.101, s32[]{:T(128)S(6)} %select_n.137), kind=kLoop, calls=%fused_computation.1 | loop fusion | flops 2097152 | bytes 3145732 | tf_op jit(solution)/shard_map/convert_element_type | solution.py:503
  123.3 4.0 %backward_prefix_kernel.1 = (f32[256,256]{1,0:T(8,128)}, f32[256,512]{1,0:T(8,128)}, f32[4,256]{1,0:T(4,128)}, f32[4,256]{1,0:T(4,128)}) custom-call(bf16[256,256]{1,0:T(8,128)(2,1)} %k_ref.11, bf16[256,512]{1,0:T(8,128)(2,1)} %v_ref.7, ...), custom_call_target="tpu_custom_call", output_to_operand_aliasing={{0}: (7, {}), {1}: (8, {}), {2}: (9, {}), {3}: (10, {})} | custom-call | flops 100000000 | bytes 1000000 | tf_op jit(solution)/shard_map/backward_prefix_kernel/pallas_call | solution.py:531
  127.3 1.6 %collective-permute-start.19 = (bf16[2,128,512]{2,1,0:T(8,128)(2,1)S(1)}, bf16[2,128,512]{2,1,0:T(8,128)(2,1)S(1)}, u32[]{:S(2)}, u32[]{:S(2)}) collective-permute-start(bf16[2,128,512]{2,1,0:T(8,128)(2,1)S(1)} %dynamic-slice_bitcast_fusion.3), channel_id=1, source_target_pairs={{0,8},{4,12},{8,0},{12,4},{16,24},{20,28},{24,16},{28,20},{1,9},{5... | collective-permute-start | bytes 786440 | tf_op jit(solution)/shard_map/ppermute | solution.py:450
  130.5 4.0 %collective-permute-done.19 = bf16[2,128,512]{2,1,0:T(8,128)(2,1)S(1)} collective-permute-done((bf16[2,128,512]{2,1,0:T(8,128)(2,1)S(1)}, bf16[2,128,512]{2,1,0:T(8,128)(2,1)S(1)}, u32[]{:S(2)}, u32[]{:S(2)}) %collective-permute-start.19) | collective-permute-done | bytes 262176 | tf_op jit(solution)/shard_map/ppermute | solution.py:450
  136.0 3.7 %collective-permute-done.20 = bf16[128,512]{1,0:T(8,128)(2,1)S(1)} collective-permute-done((bf16[128,512]{1,0:T(8,128)(2,1)S(1)}, bf16[128,512]{1,0:T(8,128)(2,1)S(1)}, u32[]{:S(2)}, u32[]{:S(2)}) %collective-permute-start.20) | collective-permute-done | bytes 131104 | tf_op jit(solution)/shard_map/ppermute | solution.py:450
  (85 shorter events, 23.2 us)
Async XLA Ops:
  0.6 53.4 %copy-start = (bf16[2048,512]{1,0:T(8,128)(2,1)S(1)}, bf16[2048,512]{1,0:T(8,128)(2,1)}, u32[]{:S(2)}) copy-start(bf16[2048,512]{1,0:T(8,128)(2,1)} %param.16) | copy-start | bytes 6291460
  7.6 25.9 %copy-start.8 = (bf16[4,128,128]{2,1,0:T(8,128)(2,1)S(1)}, bf16[4,128,128]{2,1,0:T(8,128)(2,1)}, u32[]{:S(2)}) copy-start(bf16[4,128,128]{2,1,0:T(8,128)(2,1)} %get-tuple-element.37) | copy-start | bytes 393220
  7.6 25.8 %collective-permute-start = (bf16[4,128,128]{2,1,0:T(8,128)(2,1)}, bf16[4,128,128]{2,1,0:T(8,128)(2,1)}, u32[]{:S(2)}, u32[]{:S(2)}) collective-permute-start(bf16[4,128,128]{2,1,0:T(8,128)(2,1)} %get-tuple-element.37), channel_id=1, source_target_pairs={{0,4},{4,0},{8,12},{12,8},{16,20},{20,16},{24,28},{28,24},{1,5},{5... | collective-permute-start | bytes 393224 | tf_op jit(solution)/shard_map/ppermute | solution.py:450
  8.1 28.9 %collective-permute-start.1 = (bf16[4,128,128]{2,1,0:T(8,128)(2,1)}, bf16[4,128,128]{2,1,0:T(8,128)(2,1)}, u32[]{:S(2)}, u32[]{:S(2)}) collective-permute-start(bf16[4,128,128]{2,1,0:T(8,128)(2,1)} %get-tuple-element.37), channel_id=1, source_target_pairs={{0,8},{4,12},{8,0},{12,4},{16,24},{20,28},{24,16},{28,20},{1,9},{5... | collective-permute-start | bytes 393224 | tf_op jit(solution)/shard_map/ppermute | solution.py:450
  10.6 27.7 %collective-permute-start.2 = (bf16[4,128,128]{2,1,0:T(8,128)(2,1)}, bf16[4,128,128]{2,1,0:T(8,128)(2,1)}, u32[]{:S(2)}, u32[]{:S(2)}) collective-permute-start(bf16[4,128,128]{2,1,0:T(8,128)(2,1)} %get-tuple-element.37), channel_id=1, source_target_pairs={{0,12},{4,8},{8,4},{12,0},{16,28},{20,24},{24,20},{28,16},{1,13},{... | collective-permute-start | bytes 393224 | tf_op jit(solution)/shard_map/ppermute | solution.py:450
  10.7 30.3 %collective-permute-start.3 = (bf16[4,128,128]{2,1,0:T(8,128)(2,1)}, bf16[4,128,128]{2,1,0:T(8,128)(2,1)}, u32[]{:S(2)}, u32[]{:S(2)}) collective-permute-start(bf16[4,128,128]{2,1,0:T(8,128)(2,1)} %get-tuple-element.37), channel_id=1, source_target_pairs={{0,16},{4,20},{8,24},{12,28},{16,0},{20,4},{24,8},{28,12},{1,17},{... | collective-permute-start | bytes 393224 | tf_op jit(solution)/shard_map/ppermute | solution.py:450
  12.5 32.1 %collective-permute-start.4 = (bf16[4,128,128]{2,1,0:T(8,128)(2,1)}, bf16[4,128,128]{2,1,0:T(8,128)(2,1)}, u32[]{:S(2)}, u32[]{:S(2)}) collective-permute-start(bf16[4,128,128]{2,1,0:T(8,128)(2,1)} %get-tuple-element.37), channel_id=1, source_target_pairs={{0,20},{4,16},{8,28},{12,24},{16,4},{20,0},{24,12},{28,8},{1,21},{... | collective-permute-start | bytes 393224 | tf_op jit(solution)/shard_map/ppermute | solution.py:450
  33.5 13.5 %copy-start.4 = (bf16[4,256,512]{1,2,0:T(8,128)(2,1)}, bf16[4,256,512]{1,2,0:T(8,128)(2,1)S(1)}, u32[]{:S(2)}) copy-start(bf16[4,256,512]{1,2,0:T(8,128)(2,1)S(1)} %constant_dynamic-update-slice_fusion.3) | copy-start | bytes 3145732
  33.5 13.4 %collective-permute-start.5 = (bf16[4,128,128]{2,1,0:T(8,128)(2,1)S(1)}, bf16[4,128,128]{2,1,0:T(8,128)(2,1)S(1)}, u32[]{:S(2)}, u32[]{:S(2)}) collective-permute-start(bf16[4,128,128]{2,1,0:T(8,128)(2,1)S(1)} %copy-done.8), channel_id=1, source_target_pairs={{0,24},{4,28},{8,16},{12,20},{16,8},{20,12},{24,0},{28,4},{1,25},{... | collective-permute-start | bytes 393224 | tf_op jit(solution)/shard_map/ppermute | solution.py:450
  37.1 9.9 %collective-permute-start.6 = (bf16[4,128,128]{2,1,0:T(8,128)(2,1)S(1)}, bf16[4,128,128]{2,1,0:T(8,128)(2,1)S(1)}, u32[]{:S(2)}, u32[]{:S(2)}) collective-permute-start(bf16[4,128,128]{2,1,0:T(8,128)(2,1)S(1)} %copy-done.8), channel_id=1, source_target_pairs={{0,28},{4,24},{8,20},{12,16},{16,12},{20,8},{24,4},{28,0},{1,29},{... | collective-permute-start | bytes 393224 | tf_op jit(solution)/shard_map/ppermute | solution.py:450
  38.3 17.4 %collective-permute-start.10 = (bf16[256,512]{1,0:T(8,128)(2,1)}, bf16[256,512]{1,0:T(8,128)(2,1)S(1)}, u32[]{:S(2)}, u32[]{:S(2)}) collective-permute-start(bf16[256,512]{1,0:T(8,128)(2,1)} %param.17), channel_id=1, source_target_pairs={{0,1},{1,2},{2,3},{3,0},{4,5},{5,6},{6,7},{7,4},{8,9},{9,10},{10,1... | collective-permute-start | bytes 786440 | tf_op jit(solution)/shard_map/ppermute | solution.py:454
  41.0 19.4 %collective-permute-start.11 = (bf16[256,512]{1,0:T(8,128)(2,1)}, bf16[256,512]{1,0:T(8,128)(2,1)}, u32[]{:S(2)}, u32[]{:S(2)}) collective-permute-start(bf16[256,512]{1,0:T(8,128)(2,1)} %param.17), channel_id=1, source_target_pairs={{0,2},{1,3},{2,0},{3,1},{4,6},{5,7},{6,4},{7,5},{8,10},{9,11},{10,... | collective-permute-start | bytes 786440 | tf_op jit(solution)/shard_map/ppermute | solution.py:454
  44.6 17.6 %collective-permute-start.12 = (bf16[256,512]{1,0:T(8,128)(2,1)}, bf16[256,512]{1,0:T(8,128)(2,1)}, u32[]{:S(2)}, u32[]{:S(2)}) collective-permute-start(bf16[256,512]{1,0:T(8,128)(2,1)} %param.17), channel_id=1, source_target_pairs={{0,3},{1,0},{2,1},{3,2},{4,7},{5,4},{6,5},{7,6},{8,11},{9,8},{10,9... | collective-permute-start | bytes 786440 | tf_op jit(solution)/shard_map/ppermute | solution.py:454
  47.0 1.0 copy-start.1
  55.8 0.7 copy-start.7
  70.8 17.1 %copy-start.6 = (bf16[256,512]{1,0:T(8,128)(2,1)S(1)}, bf16[256,512]{1,0:T(8,128)(2,1)}, u32[]{:S(2)}) copy-start(bf16[256,512]{1,0:T(8,128)(2,1)} %get-tuple-element.38) | copy-start | bytes 786436
  77.3 10.6 %copy-start.5 = (bf16[4,256,512]{1,2,0:T(8,128)(2,1)S(1)}, bf16[4,256,512]{1,2,0:T(8,128)(2,1)}, u32[]{:S(2)}) copy-start(bf16[4,256,512]{1,2,0:T(8,128)(2,1)} %constant_dynamic-update-slice_fusion) | copy-start | bytes 3145732
  79.3 17.8 %collective-permute-start.13 = (bf16[2,2,512,128]{3,2,1,0:T(8,128)(2,1)}, bf16[2,2,512,128]{3,2,1,0:T(8,128)(2,1)}, u32[]{:S(2)}, u32[]{:S(2)}) collective-permute-start(bf16[2,2,512,128]{3,2,1,0:T(8,128)(2,1)} %dynamic-slice_bitcast_fusion.1), channel_id=1, source_target_pairs={{0,4},{4,0},{8,12},{12,8},{16,20},{20,16},{24,28},{28,24},{1,5},{5... | collective-permute-start | bytes 1572872 | tf_op jit(solution)/shard_map/ppermute | solution.py:450
  80.2 19.9 %collective-permute-start.9 = (bf16[256,512]{1,0:T(8,128)(2,1)}, bf16[256,512]{1,0:T(8,128)(2,1)}, u32[]{:S(2)}, u32[]{:S(2)}) collective-permute-start(bf16[256,512]{1,0:T(8,128)(2,1)} %get-tuple-element.61), channel_id=1, source_target_pairs={{0,3},{1,0},{2,1},{3,2},{4,7},{5,4},{6,5},{7,6},{8,11},{9,8},{10,9... | collective-permute-start | bytes 786440 | tf_op jit(solution)/shard_map/ppermute | solution.py:454
  87.3 22.5 %collective-permute-start.8 = (bf16[256,512]{1,0:T(8,128)(2,1)}, bf16[256,512]{1,0:T(8,128)(2,1)}, u32[]{:S(2)}, u32[]{:S(2)}) collective-permute-start(bf16[256,512]{1,0:T(8,128)(2,1)} %get-tuple-element.62), channel_id=1, source_target_pairs={{0,2},{1,3},{2,0},{3,1},{4,6},{5,7},{6,4},{7,5},{8,10},{9,11},{10,... | collective-permute-start | bytes 786440 | tf_op jit(solution)/shard_map/ppermute | solution.py:454
  87.3 22.5 %collective-permute-start.7 = (bf16[256,512]{1,0:T(8,128)(2,1)}, bf16[256,512]{1,0:T(8,128)(2,1)}, u32[]{:S(2)}, u32[]{:S(2)}) collective-permute-start(bf16[256,512]{1,0:T(8,128)(2,1)} %get-tuple-element.60), channel_id=1, source_target_pairs={{0,1},{1,2},{2,3},{3,0},{4,5},{5,6},{6,7},{7,4},{8,9},{9,10},{10,1... | collective-permute-start | bytes 786440 | tf_op jit(solution)/shard_map/ppermute | solution.py:454
  88.6 1.4 copy-start.2
  91.0 28.3 %collective-permute-start.18 = (bf16[2,2,256,512]{3,2,1,0:T(8,128)(2,1)}, bf16[2,2,256,512]{3,2,1,0:T(8,128)(2,1)}, u32[]{:S(2)}, u32[]{:S(2)}) collective-permute-start(bf16[2,2,256,512]{3,2,1,0:T(8,128)(2,1)} %dynamic-slice_bitcast_fusion), channel_id=1, source_target_pairs={{0,4},{4,0},{8,12},{12,8},{16,20},{20,16},{24,28},{28,24},{1,5},{5... | collective-permute-start | bytes 3145736 | tf_op jit(solution)/shard_map/ppermute | solution.py:450
  98.4 20.9 %copy-start.3 = (bf16[4,512,512]{2,1,0:T(8,128)(2,1)S(1)}, bf16[4,512,512]{2,1,0:T(8,128)(2,1)}, u32[]{:S(2)}) copy-start(bf16[4,512,512]{2,1,0:T(8,128)(2,1)} %copy-done.2) | copy-start | bytes 6291460
  98.5 14.9 %collective-permute-start.16 = (bf16[2,256,128]{2,1,0:T(8,128)(2,1)S(1)}, bf16[2,256,128]{2,1,0:T(8,128)(2,1)S(1)}, u32[]{:S(2)}, u32[]{:S(2)}) collective-permute-start(bf16[2,256,128]{2,1,0:T(8,128)(2,1)S(1)} %dynamic-slice_bitcast_fusion.9), channel_id=1, source_target_pairs={{0,16},{4,20},{8,24},{12,28},{16,0},{20,4},{24,8},{28,12},{1,17},{... | collective-permute-start | bytes 393224 | tf_op jit(solution)/shard_map/ppermute | solution.py:450
  111.8 5.8 %collective-permute-start.14 = (bf16[2,256,128]{2,1,0:T(8,128)(2,1)S(1)}, bf16[2,256,128]{2,1,0:T(8,128)(2,1)S(1)}, u32[]{:S(2)}, u32[]{:S(2)}) collective-permute-start(bf16[2,256,128]{2,1,0:T(8,128)(2,1)S(1)} %dynamic-slice_bitcast_fusion.10), channel_id=1, source_target_pairs={{0,8},{4,12},{8,0},{12,4},{16,24},{20,28},{24,16},{28,20},{1,9},{5... | collective-permute-start | bytes 393224 | tf_op jit(solution)/shard_map/ppermute | solution.py:450
  113.4 5.8 %collective-permute-start.17 = (bf16[256,128]{1,0:T(8,128)(2,1)S(1)}, bf16[256,128]{1,0:T(8,128)(2,1)S(1)}, u32[]{:S(2)}, u32[]{:S(2)}) collective-permute-start(bf16[256,128]{1,0:T(8,128)(2,1)S(1)} %dynamic-slice_bitcast_fusion.11), channel_id=1, source_target_pairs={{0,8},{4,12},{8,0},{12,4},{16,24},{20,28},{24,16},{28,20},{1,9},{5... | collective-permute-start | bytes 196616 | tf_op jit(solution)/shard_map/ppermute | solution.py:450
  117.7 4.9 %collective-permute-start.15 = (bf16[256,128]{1,0:T(8,128)(2,1)S(1)}, bf16[256,128]{1,0:T(8,128)(2,1)S(1)}, u32[]{:S(2)}, u32[]{:S(2)}) collective-permute-start(bf16[256,128]{1,0:T(8,128)(2,1)S(1)} %dynamic-slice_bitcast_fusion.12), channel_id=1, source_target_pairs={{0,16},{4,20},{8,24},{12,28},{16,0},{20,4},{24,8},{28,12},{1,17},{... | collective-permute-start | bytes 196616 | tf_op jit(solution)/shard_map/ppermute | solution.py:450
  120.9 8.0 %collective-permute-start.21 = (bf16[2,128,512]{2,1,0:T(8,128)(2,1)S(1)}, bf16[2,128,512]{2,1,0:T(8,128)(2,1)}, u32[]{:S(2)}, u32[]{:S(2)}) collective-permute-start(bf16[2,128,512]{2,1,0:T(8,128)(2,1)S(1)} %dynamic-slice_bitcast_fusion.2), channel_id=1, source_target_pairs={{0,16},{4,20},{8,24},{12,28},{16,0},{20,4},{24,8},{28,12},{1,17},{... | collective-permute-start | bytes 786440 | tf_op jit(solution)/shard_map/ppermute | solution.py:450
  127.3 7.2 %collective-permute-start.19 = (bf16[2,128,512]{2,1,0:T(8,128)(2,1)S(1)}, bf16[2,128,512]{2,1,0:T(8,128)(2,1)S(1)}, u32[]{:S(2)}, u32[]{:S(2)}) collective-permute-start(bf16[2,128,512]{2,1,0:T(8,128)(2,1)S(1)} %dynamic-slice_bitcast_fusion.3), channel_id=1, source_target_pairs={{0,8},{4,12},{8,0},{12,4},{16,24},{20,28},{24,16},{28,20},{1,9},{5... | collective-permute-start | bytes 786440 | tf_op jit(solution)/shard_map/ppermute | solution.py:450
  129.9 6.0 %collective-permute-start.22 = (bf16[128,512]{1,0:T(8,128)(2,1)S(1)}, bf16[128,512]{1,0:T(8,128)(2,1)S(1)}, u32[]{:S(2)}, u32[]{:S(2)}) collective-permute-start(bf16[128,512]{1,0:T(8,128)(2,1)S(1)} %dynamic-slice_bitcast_fusion.7), channel_id=1, source_target_pairs={{0,8},{4,12},{8,0},{12,4},{16,24},{20,28},{24,16},{28,20},{1,9},{5... | collective-permute-start | bytes 393224 | tf_op jit(solution)/shard_map/ppermute | solution.py:450
  134.7 5.0 %collective-permute-start.20 = (bf16[128,512]{1,0:T(8,128)(2,1)S(1)}, bf16[128,512]{1,0:T(8,128)(2,1)S(1)}, u32[]{:S(2)}, u32[]{:S(2)}) collective-permute-start(bf16[128,512]{1,0:T(8,128)(2,1)S(1)} %dynamic-slice_bitcast_fusion.8), channel_id=1, source_target_pairs={{0,16},{4,20},{8,24},{12,28},{16,0},{20,4},{24,8},{28,12},{1,17},{... | collective-permute-start | bytes 393224 | tf_op jit(solution)/shard_map/ppermute | solution.py:450
